TPU v7x, 256 devices: a whole 4x4x8 slice. The times are simulated.
256 devices in a mesh: blk: 16 (over x_lo, z), tgt: 16 (over y, x_hi, core).
Axes of the slice: x: 4 (x_hi: 2, x_lo: 2; x = x_hi * 2 + x_lo), y: 4, z: 8, core: 2. Of those that a mesh axis runs over, the one named last changes fastest.
Arguments:
- sources: float32 [16384, 128], P('blk'), may hold values from -0.5 to 0.5, as said below
- targets: float32 [65536, 128], P(('blk', 'tgt')), may hold values from -0.5 to 0.5, as said below
- duals_init: float32 [65536], P(('blk', 'tgt')), may hold values from -1.5 to 1.5
Outputs:
- source_duals: float32 [16384], P('blk')
- target_duals: float32 [65536], P(('blk', 'tgt'))
Inputs may be any that keep to these rules, and one draw needn't show every extreme that they name: `sources`: coordinates of the source points. `targets`: coordinates of the target points.
All inputs are finite; a program needn't handle non-finite values.
Results may differ from a plain program's by a relative error of at most 0.0001.
Values sent between devices are 32-bit elements; how exact they have to be, the bound alone decides.
No kernel may reach another device: no remote copies, remote signals or barrier semaphores. Data moves between devices by JAX's collectives and lax.ppermute only.
A program may use at most 64 MiB of HBM per device.

v0:
```python
import jax
import jax.numpy as jnp
from jax import lax
from jax.sharding import Mesh
from jax.sharding import PartitionSpec as P

ITERS = 2
BLK = ("blk_0", "blk_1")
BLK_TGT = ("blk_0", "blk_1", "tgt")


EPS = 0.05


def in_order(blocks, dim):
    shape = list(blocks.shape[1:])
    shape[dim] *= blocks.shape[0]
    return jnp.moveaxis(blocks, 0, dim).reshape(shape)


def all_blocks(x, axes, turns):
    blocks = x
    for k in turns:
        blocks = lax.all_gather(blocks, axes[k])
    done = turns[::-1]
    back = [done.index(k) for k in range(len(axes))]
    blocks = blocks.transpose(*back, *range(len(axes), blocks.ndim))
    return blocks.reshape(-1, *x.shape)


def gather_axes(x, axes, turns, dim):
    return in_order(all_blocks(x, axes, turns), dim)


def sent_to_all(x, axis):
    count = lax.axis_size(axis)
    return lax.all_to_all(jnp.broadcast_to(x[None], (count, *x.shape)), axis, 0, 0, tiled=True)


def collect(x, axis, dim):
    return in_order(sent_to_all(x, axis), dim)


def gathered_once(x, axis):
    leaves = jax.tree.leaves(x)
    turns = sorted(range(len(leaves)), key=lambda k: -leaves[k].size)
    width = (1, *leaves[turns[0]].shape)[-1]
    lines = [
        jnp.pad(leaves[k].reshape(-1), (0, -leaves[k].size % width)).reshape(-1, width)
        for k in turns
    ]
    both, at, found = (sent_to_all(jnp.concatenate(lines), axis), 0, {})
    for k, line in zip(turns, lines):
        section = both[:, at : at + len(line)].reshape(len(both), -1)
        found[k] = section[:, : leaves[k].size].reshape(-1, *leaves[k].shape)
        at += len(line)
    numbers = iter(range(len(leaves)))
    return jax.tree.map(lambda _: found[next(numbers)], x)


def gathered_by_type(x, axis):
    leaves, found = (jax.tree.leaves(x), {})
    for first, a in enumerate(leaves):
        if first not in found:
            alike = [k for k, b in enumerate(leaves) if b.dtype == a.dtype]
            got = (
                gathered_once([leaves[k] for k in alike], axis)
                if len(alike) > 1
                else [sent_to_all(a, axis)]
            )
            for k, b in zip(alike, got):
                found[k] = b
    numbers = iter(range(len(leaves)))
    return jax.tree.map(lambda _: found[next(numbers)], x)


def folded_in_pairs(pieces, combine):
    while len(jax.tree.leaves(pieces)[0]) > 1:
        pieces = jax.vmap(combine)(
            *(jax.tree.map(lambda part: part[side::2], pieces) for side in (0, 1))
        )
    return jax.tree.map(lambda part: part[0], pieces)


def joined_all(x, axis, combine):
    pieces = gathered_by_type(x, axis)
    return folded_in_pairs(pieces, combine)


def over_copies(x, axis):
    everything = sent_to_all(x, axis)
    return jnp.max(everything, axis=0)


def split_up(x, dim, count):
    shape = x.shape
    blocks = x.reshape(*shape[:dim], count, shape[dim] // count, *shape[dim + 1 :])
    return jnp.moveaxis(blocks, dim, 0)


def sent_and_summed(x, axis, dim):
    count = lax.axis_size(axis)
    blocks = lax.all_to_all(split_up(x, dim, count), axis, 0, 0, tiled=True)
    return jnp.sum(blocks, axis=0)


def cost_of(left, left_norm, right, right_norm):
    cross = jnp.dot(
        left, right.T, preferred_element_type=jnp.float32, precision=lax.Precision.HIGHEST
    )
    return left_norm[:, None] + right_norm[None, :] - 2.0 * cross


def combine(first, second):
    highest = jnp.maximum(first[0], second[0])
    return (
        highest,
        first[1] * jnp.exp(first[0] - highest) + second[1] * jnp.exp(second[0] - highest),
    )


def body(sources, targets, duals_init):
    src_norm = jnp.sum(sources * sources, axis=1)
    rows_here = sources.shape[0]
    cols_here = targets.shape[0]
    total_dst = cols_here * lax.axis_size(BLK) * lax.axis_size("tgt")
    total_src = rows_here * lax.axis_size(BLK)
    target_pots = duals_init
    source_pots = jnp.zeros_like(src_norm)
    group_rows = gather_axes(targets, BLK, (0, 1), 0)
    group_norm = jnp.sum(group_rows * group_rows, axis=1)
    cost_tile = cost_of(sources, src_norm, group_rows, group_norm)
    for repeat in range(ITERS):
        group_pots = collect(target_pots, BLK, 0)
        scores = (group_pots[None, :] - cost_tile) / EPS
        maxima = jnp.max(scores, axis=1)
        totals = jnp.sum(jnp.exp(scores - maxima[:, None]), axis=1)
        maxima, totals = joined_all((maxima, totals), "tgt", combine)
        source_pots = EPS * -jnp.log(jnp.float32(total_dst)) - EPS * (maxima + jnp.log(totals))
        col_scores = (source_pots[:, None] - cost_tile) / EPS
        col_high = over_copies(jnp.max(col_scores, axis=0), BLK)
        col_part = jnp.sum(jnp.exp(col_scores - col_high[None, :]), axis=0)
        col_total = sent_and_summed(col_part, BLK, 0)
        own_high = lax.dynamic_slice_in_dim(col_high, lax.axis_index(BLK) * cols_here, cols_here, 0)
        target_pots = EPS * -jnp.log(jnp.float32(total_src)) - EPS * (own_high + jnp.log(col_total))
    return (source_pots, target_pots)


def solution(mesh):
    finer = Mesh(mesh.devices.reshape(2, 8, mesh.shape["tgt"]), ("blk_0", "blk_1", "tgt"))
    return jax.shard_map(
        body,
        mesh=finer,
        in_specs=(P(BLK, None), P(BLK_TGT, None), P(BLK_TGT)),
        out_specs=(P(BLK), P(BLK_TGT)),
        check_vma=False,
    )
```

profile of v0, /device:TPU:1, one launch (start us, length us, event | category | flops | bytes accessed | tf_op | source)
XLA Modules:
  0.0 236.0 jit_solution(17945655105315867702)
XLA Ops:
  7.2 6.9 %all-gather = f32[512,128]{1,0:T(8,128)} all-gather(f32[256,128]{1,0:T(8,128)} %param.4), channel_id=2, replica_groups=mesh['blk_0'=2,'blk_1'=8,'tgt'=16] {'blk_0'}, dimensions={0}, use_global_device_ids=true | all-gather | bytes 393216 | tf_op jit(solution)/shard_map/all_gather | solution.py:24
  14.1 1.3 broadcast_in_dim.12
  15.4 9.1 %all-to-all-start = ((f32[16,1,256]{2,1,0:T(1,128)}), f32[16,1,256]{2,1,0:T(1,128)S(1)}, u32[]{:S(2)}, u32[]{:S(2)}) async-start(f32[16,1,256]{2,1,0:T(1,128)} %broadcast_in_dim.12), calls=%async_computation | async-start | bytes 32768 | tf_op jit(solution)/shard_map/all_to_all | solution.py:37
  24.6 1.2 multiply_reduce_fusion.1
  25.8 29.2 %all-gather.4.cloned.1.call-done = f32[16,256,128]{2,1,0:T(8,128)} async-done(((f32[2,256,128]{2,1,0:T(8,128)}), f32[16,256,128]{2,1,0:T(8,128)}) %all-gather.4.cloned.1.call-update) | async-done | bytes 2097168 | tf_op jit(solution)/shard_map/all_gather | solution.py:24
  55.1 2.2 multiply_reduce_fusion
  57.3 1.7 copy.21
  59.1 17.7 %fusion = (f32[1024]{0:T(1024)S(1)}, f32[1024,4096]{1,0:T(8,128)S(1)}) fusion(f32[4096]{0:T(1024)S(1)} %bitcast.41, f32[1024,128]{1,0:T(8,128)} %param.3, f32[4096,128]{1,0:T(8,128)S(1)} %bitcast.33, f32[4096]{0:T(1024)S(1)} %bitcast.54, f32[1024]{0:T(1024)S(1)} %multiply_reduce_fusion.1), kind=kOutput, calls=%fused_computation.9 | convolution fusion | flops 6467615744 | bytes 19439616 | tf_op jit(solution)/shard_map/dot_general | solution.py:108
  76.7 5.7 %copy-done = f32[1024,4096]{1,0:T(8,128)} copy-done((f32[1024,4096]{1,0:T(8,128)}, f32[1024,4096]{1,0:T(8,128)S(1)}, u32[]{:S(2)}) %copy-start) | copy-done | bytes 16777240
  82.5 4.1 %exponential_reduce_fusion.3 = f32[1024]{0:T(1024)S(1)} fusion(f32[1024,4096]{1,0:T(8,128)S(1)} %get-tuple-element.19, f32[1024]{0:T(1024)S(1)} %get-tuple-element.18, f32[4096]{0:T(1024)S(1)} %bitcast.42), kind=kLoop, calls=%fused_computation.6 | loop fusion | flops 16776192 | bytes 16801792 | tf_op jit(solution)/shard_map/reduce_sum | solution.py:137
  86.6 19.0 %all_to_all.52 = f32[16,2,1024]{2,1,0:T(2,128)S(1)} all-to-all(f32[16,2,1024]{2,1,0:T(2,128)S(1)} %broadcast_in_dim.13), channel_id=1, replica_groups=mesh['blk_0'=2,'blk_1'=8,'tgt'=16] {'tgt'}, dimensions={0} | all-to-all | bytes 262144 | tf_op jit(solution)/shard_map/all_to_all | solution.py:37
  105.6 0.1 fusion.9
  106.1 7.7 %fusion.1 = f32[4096]{0:T(1024)S(1)} fusion(f32[1024,4096]{1,0:T(8,128)} %copy-done, f32[1024]{0:T(1024)S(1)} %bitcast.48), kind=kLoop, calls=%fused_computation.10 | loop fusion | flops 12578816 | bytes 16797696 | tf_op jit(solution)/shard_map/reduce_max | solution.py:141
  113.9 0.2 broadcast_in_dim.14
  114.1 12.7 %all_to_all.53 = f32[16,1,4096]{2,1,0:T(1,128)S(1)} all-to-all(f32[16,1,4096]{2,1,0:T(1,128)S(1)} %broadcast_in_dim.14), channel_id=1, replica_groups=mesh['blk_0'=2,'blk_1'=8,'tgt'=16] {'blk_0','blk_1'}, dimensions={0} | all-to-all | bytes 524288 | tf_op jit(solution)/shard_map/all_to_all | solution.py:37
  126.8 0.2 reduce_max.56
  126.9 8.3 %exponential_reduce_fusion.2 = f32[4096]{0:T(1024)} fusion(f32[1024,4096]{1,0:T(8,128)} %copy-done, f32[4096]{0:T(1024)S(1)} %reduce_max.56, f32[1024]{0:T(1024)S(1)} %bitcast.49), kind=kLoop, calls=%fused_computation.4 | loop fusion | flops 16773120 | bytes 16814080 | tf_op jit(solution)/shard_map/reduce_sum | solution.py:142
  135.3 5.4 %all-to-all-start.3 = ((f32[16,1,256]{2,1,0:T(1,128)}), f32[16,1,256]{2,1,0:T(1,128)S(1)}, u32[]{:S(2)}, u32[]{:S(2)}) async-start(f32[16,1,256]{2,1,0:T(1,128)} %bitcast.10), calls=%async_computation.3 | async-start | bytes 32768 | tf_op jit(solution)/shard_map/all_to_all | solution.py:103
  140.7 7.3 %all-to-all-done.3 = f32[16,1,256]{2,1,0:T(1,128)S(1)} async-done(((f32[16,1,256]{2,1,0:T(1,128)}), f32[16,1,256]{2,1,0:T(1,128)S(1)}, u32[]{:S(2)}, u32[]{:S(2)}) %all-to-all-start.3) | async-done | bytes 16416 | tf_op jit(solution)/shard_map/all_to_all | solution.py:103
  148.1 0.1 multiply_subtract_fusion.4
  148.2 9.9 %all_to_all.54 = f32[16,1,256]{2,1,0:T(1,128)S(1)} all-to-all(f32[16,1,256]{2,1,0:T(1,128)S(1)} %broadcast_in_dim.15), channel_id=1, replica_groups=mesh['blk_0'=2,'blk_1'=8,'tgt'=16] {'blk_0','blk_1'}, dimensions={0} | all-to-all | bytes 32768 | tf_op jit(solution)/shard_map/all_to_all | solution.py:37
  158.1 7.6 %fusion.2 = f32[1024]{0:T(1024)S(1)} fusion(f32[1024,4096]{1,0:T(8,128)} %copy-done, f32[4096]{0:T(1024)S(1)} %bitcast.39), kind=kLoop, calls=%fused_computation.11 | loop fusion | flops 12581888 | bytes 16797696 | tf_op jit(solution)/shard_map/reduce_max | solution.py:136
  165.6 7.9 %exponential_reduce_fusion.1 = f32[1024]{0:T(1024)S(1)} fusion(f32[1024,4096]{1,0:T(8,128)} %copy-done, f32[1024]{0:T(1024)S(1)} %fusion.2, f32[4096]{0:T(1024)S(1)} %bitcast.40), kind=kLoop, calls=%fused_computation.2 | loop fusion | flops 16776192 | bytes 16801792 | tf_op jit(solution)/shard_map/reduce_sum | solution.py:137
  173.6 14.4 %all_to_all.55 = f32[16,2,1024]{2,1,0:T(2,128)S(1)} all-to-all(f32[16,2,1024]{2,1,0:T(2,128)S(1)} %broadcast_in_dim.16), channel_id=1, replica_groups=mesh['blk_0'=2,'blk_1'=8,'tgt'=16] {'tgt'}, dimensions={0} | all-to-all | bytes 262144 | tf_op jit(solution)/shard_map/all_to_all | solution.py:37
  187.9 0.1 fusion.8
  188.5 7.7 %fusion.3 = f32[4096]{0:T(1024)S(1)} fusion(f32[1024,4096]{1,0:T(8,128)} %copy-done, f32[1024]{0:T(1024)S(1)} %bitcast.45), kind=kLoop, calls=%fused_computation.12 | loop fusion | flops 12578816 | bytes 16797696 | tf_op jit(solution)/shard_map/reduce_max | solution.py:141
  196.2 0.2 broadcast_in_dim.17
  196.4 11.6 %all_to_all.56 = f32[16,1,4096]{2,1,0:T(1,128)S(1)} all-to-all(f32[16,1,4096]{2,1,0:T(1,128)S(1)} %broadcast_in_dim.17), channel_id=1, replica_groups=mesh['blk_0'=2,'blk_1'=8,'tgt'=16] {'blk_0','blk_1'}, dimensions={0} | all-to-all | bytes 524288 | tf_op jit(solution)/shard_map/all_to_all | solution.py:37
  208.0 0.2 reduce_max.59
  208.2 7.7 %exponential_reduce_fusion = f32[4096]{0:T(1024)S(1)} fusion(f32[1024,4096]{1,0:T(8,128)} %copy-done, f32[4096]{0:T(1024)S(1)} %reduce_max.59, f32[1024]{0:T(1024)S(1)} %bitcast.46), kind=kLoop, calls=%fused_computation | loop fusion | flops 16773120 | bytes 16814080 | tf_op jit(solution)/shard_map/reduce_sum | solution.py:142
  216.0 12.5 %all_to_all.57 = f32[16,1,256]{2,1,0:T(1,128)S(1)} all-to-all(f32[16,1,256]{2,1,0:T(1,128)S(1)} %bitcast.43), channel_id=1, replica_groups=mesh['blk_0'=2,'blk_1'=8,'tgt'=16] {'blk_0','blk_1'}, dimensions={0} | all-to-all | bytes 32768 | tf_op jit(solution)/shard_map/all_to_all | solution.py:103
  228.5 0.6 multiply_subtract_fusion.3
  (50 shorter events, 1.1 us)
Async XLA Ops:
  7.2 47.9 %all-gather.4.cloned.1.call-start = ((), (), s32[]{:S(2)}) async-start(), calls=%async_computation.8 | async-start | bytes 2359296 | tf_op jit(solution)/shard_map/all_gather | solution.py:24
  15.4 43.6 %all-to-all-start = ((f32[16,1,256]{2,1,0:T(1,128)}), f32[16,1,256]{2,1,0:T(1,128)S(1)}, u32[]{:S(2)}, u32[]{:S(2)}) async-start(f32[16,1,256]{2,1,0:T(1,128)} %broadcast_in_dim.12), calls=%async_computation | async-start | bytes 32768 | tf_op jit(solution)/shard_map/all_to_all | solution.py:37
  76.7 5.7 %copy-start = (f32[1024,4096]{1,0:T(8,128)}, f32[1024,4096]{1,0:T(8,128)S(1)}, u32[]{:S(2)}) copy-start(f32[1024,4096]{1,0:T(8,128)S(1)} %get-tuple-element.19) | copy-start | bytes 50331652
  135.3 12.8 %all-to-all-start.3 = ((f32[16,1,256]{2,1,0:T(1,128)}), f32[16,1,256]{2,1,0:T(1,128)S(1)}, u32[]{:S(2)}, u32[]{:S(2)}) async-start(f32[16,1,256]{2,1,0:T(1,128)} %bitcast.10), calls=%async_computation.3 | async-start | bytes 32768 | tf_op jit(solution)/shard_map/all_to_all | solution.py:103
  188.5 27.5 %copy-start.1 = (f32[1,1024]{1,0:T(1,128)}, f32[1,1024]{1,0:T(1,128)S(1)}, u32[]{:S(2)}) copy-start(f32[1,1024]{1,0:T(1,128)S(1)} %multiply_subtract_fusion.1) | copy-start | bytes 12292
Sparse Core Ops, SparseCore 0:
  14.3 40.7 all-gather.3
where the time goes:
time: 237 us; the launch traced here: 236 us
  blocking collectives  86.9 us (37%)
  other arithmetic  55.9 us (24%)
  waiting for transfers between devices  36.6 us (15%)
  matrix products  17.7 us (7%)
  starting transfers between devices  14.6 us (6%)
  between operations  14.3 us (6%)
  local copies, waits for them, and re-layouts  10 us (4%)
    all_to_all x5, blocking collectives, sent_to_all(): lax.all_to_all(jnp.broadcast_to(x[None], (count, *x.shape)), axis, 0, 0,...  67.5 us
    all_gather x1, waiting for transfers between devices, all_blocks(): blocks = lax.all_gather(blocks, axes[k])  29.2 us
    dot_general x1, matrix products, cost_of(): jnp.dot(left, right.T, preferred_element_type=jnp.float32, precision=lax....  17.7 us
    reduce_sum x2, other arithmetic, body(): col_part = jnp.sum(jnp.exp(col_scores - col_high[None, :]), axis=0)  16.1 us
    reduce_max x2, other arithmetic, body(): col_high = over_copies(jnp.max(col_scores, axis=0), BLK)  15.4 us
    all_to_all x1, blocking collectives, sent_and_summed(): blocks = lax.all_to_all(split_up(x, dim, count), axis, 0, 0, tiled=True)  12.5 us
    reduce_sum x2, other arithmetic, body(): totals = jnp.sum(jnp.exp(scores - maxima[:, None]), axis=1)  12 us
    all_to_all x1, starting transfers between devices, sent_to_all(): lax.all_to_all(jnp.broadcast_to(x[None], (count, *x.shape)), axis, 0, 0,...  9.13 us
  transfers between devices with their start and end apart: 3, of which 2 were waited for; matrix products, arithmetic and copies ran while one was open for 3% of the time, Pallas kernels for 0%

commit v1 on v0

v1 whole, which is shorter than its diff:
```python
import functools
import math

import jax
import jax.numpy as jnp
from jax import lax
from jax.experimental import pallas as pl
from jax.experimental.pallas import tpu as pltpu
from jax.sharding import Mesh
from jax.sharding import PartitionSpec as P

EPS = 0.05
SCALE = math.log2(math.e) / EPS
LOG2E = math.log2(math.e)
N_SRC = 16384
N_DST = 65536
ROWS = 1024
COLS = 256
RING = 8
PLANE = 32
WIDE = 2 * ROWS
PACK = COLS + 8
OFFSETS = (0, -1, 1, -2, 2, -3, 3, -4)
GROUPS = (3, 2, 2, 1)
MIB = 1024 * 1024

BLK = ("xl", "z")
TGT = ("y", "xh", "core")
PLANE_AXES = ("xl", "y", "xh", "core")

VMEM = pl.BlockSpec(memory_space=pltpu.VMEM)
SMEM = pl.BlockSpec(memory_space=pltpu.SMEM)


def log2(x):
    return jnp.log(x) * LOG2E


def diagonal():
    shape = (128, 128)
    return lax.broadcasted_iota(jnp.int32, shape, 0) == lax.broadcasted_iota(jnp.int32, shape, 1)


def as_column(eye, row):
    return jnp.sum(jnp.where(eye, row, 0.0), axis=1, keepdims=True)


def as_row(eye, column):
    return jnp.sum(jnp.where(eye, column, 0.0), axis=0, keepdims=True)


def tree(op, parts):
    parts = list(parts)
    while len(parts) > 1:
        parts = [op(*parts[k : k + 2]) if k + 1 < len(parts) else parts[k] for k in range(0, len(parts), 2)]
    return parts[0]


def three_parts(x):
    high = x.astype(jnp.bfloat16)
    rest = x - high.astype(jnp.float32)
    mid = rest.astype(jnp.bfloat16)
    low = (rest - mid.astype(jnp.float32)).astype(jnp.bfloat16)
    return high, mid, low


def online(scores, state):
    high = jnp.max(scores, axis=0)
    if state is None:
        return high, jnp.sum(jnp.exp2(scores - high[None]), axis=0)
    high = jnp.maximum(high, state[0])
    total = state[1] * jnp.exp2(state[0] - high) + jnp.sum(jnp.exp2(scores - high[None]), axis=0)
    return high, total


def over_sublanes(high, total):
    top = jnp.max(high, axis=0, keepdims=True)
    return top + log2(jnp.sum(total * jnp.exp2(high - top), axis=0, keepdims=True))


def joined(parts):
    top = jnp.max(parts, axis=0)
    return top + log2(jnp.sum(jnp.exp2(parts - top[None]), axis=0))


def put_rows(where_ref, rows_ref, lse_tiles):
    mine = where_ref[1]
    halves = [jnp.concatenate(lse_tiles[8 * h : 8 * h + 8], axis=0) for h in range(2)]
    for h in range(2):
        half = mine if h == 0 else 1 - mine
        for peer in range(PLANE):
            rows_ref[peer, half] = halves[h]


def build_kernel(first, last, count, *refs):
    refs = list(refs)
    where_ref = refs.pop(0)
    if first:
        sources = refs.pop(0), refs.pop(0)
    else:
        x_ref, high_in, total_in = refs.pop(0), refs.pop(0), refs.pop(0)
    blocks = [refs.pop(0) for _ in range(count)]
    tile_ref = refs.pop(0)
    if first:
        x_ref, src_norm_ref, dst_norm_ref = refs.pop(0), refs.pop(0), refs.pop(0)
    if last:
        rows_ref = refs.pop(0)
    else:
        high_out, total_out = refs.pop(0), refs.pop(0)
    eye = diagonal()
    if first:
        for h in range(2):
            x = sources[h][...]
            high, mid, low = three_parts(x * (2.0 * SCALE))
            x_ref[h * ROWS : (h + 1) * ROWS, :] = jnp.concatenate([high, high, mid, mid, low, high], axis=1)
            if h == 0:
                norms = jnp.sum(x * x, axis=1, keepdims=True)
                for c in range(ROWS // 128):
                    src_norm_ref[c : c + 1, :] = as_row(eye, norms[c * 128 : (c + 1) * 128])
    parts, starts = [], []
    for b in range(count):
        y = blocks[b][0:COLS, :]
        norms = jnp.sum(y * y, axis=1, keepdims=True)
        if first and b == 0:
            for c in range(COLS // 128):
                dst_norm_ref[c : c + 1, :] = as_row(eye, norms[c * 128 : (c + 1) * 128])
        pots = [as_column(eye, blocks[b][COLS + c : COLS + c + 1, :]) for c in range(COLS // 128)]
        starts.append((jnp.concatenate(pots, axis=0) - norms) * SCALE)
        high, mid, low = three_parts(y)
        parts.append(jnp.concatenate([high, mid, high, mid, high, low], axis=1))
    step = 512
    lse_tiles = []
    for a in range(WIDE // step):
        lanes = slice(a * step, (a + 1) * step)
        state = None if first else (high_in[:, lanes], total_in[:, lanes])
        for b in range(count):
            piece = lax.dot_general(
                parts[b], x_ref[lanes, :], (((1,), (1,)), ((), ())), preferred_element_type=jnp.float32
            )
            tile_ref[b, :, lanes] = piece
            state = online((piece + starts[b]).reshape(COLS // 8, 8, step), state)
        if last:
            done = over_sublanes(*state)
            lse_tiles += [done[:, k * 128 : (k + 1) * 128] for k in range(step // 128)]
        else:
            high_out[:, lanes], total_out[:, lanes] = state
    if last:
        put_rows(where_ref, rows_ref, lse_tiles)


def build(where, count, blocks, sources=None, state=None, last=False):
    first = sources is not None
    args = [where, *(sources if first else state), *blocks]
    f32, bf16 = jnp.float32, jnp.bfloat16
    outs = [jax.ShapeDtypeStruct((count, COLS, WIDE), f32)]
    if first:
        outs += [
            jax.ShapeDtypeStruct((WIDE, 768), bf16),
            jax.ShapeDtypeStruct((ROWS // 128, 128), f32),
            jax.ShapeDtypeStruct((COLS // 128, 128), f32),
        ]
    if last:
        outs.append(jax.ShapeDtypeStruct((PLANE, 2, ROWS // 128, 128), f32))
    else:
        outs += [jax.ShapeDtypeStruct((8, WIDE), f32)] * 2
    return pl.pallas_call(
        functools.partial(build_kernel, first, last, count),
        out_shape=outs,
        in_specs=[SMEM] + [VMEM] * (len(args) - 1),
        out_specs=[VMEM] * len(outs),
        compiler_params=pltpu.CompilerParams(vmem_limit_bytes=28 * MIB),
        cost_estimate=pl.CostEstimate(
            flops=2 * count * COLS * WIDE * 768, bytes_accessed=4 * MIB, transcendentals=count * COLS * WIDE
        ),
        name=f"build_{count}_{int(first)}{int(last)}",
    )(*args)


def tile_blocks(tiles):
    return [(tiles[g], b) for g, count in enumerate(GROUPS) for b in range(count)]


def columns_kernel(copies, where_ref, rows_ref, src_norm_ref, *refs):
    tiles, refs = refs[: len(GROUPS)], refs[len(GROUPS) :]
    if copies:
        cols_ref, high_scr, total_scr = refs
    else:
        cols_ref, source_pots_ref, high_scr, total_scr = refs
    z, mine = where_ref[0], where_ref[1]
    eye = diagonal()
    pots = []
    for h in range(2):
        half = mine if h == 0 else 1 - mine
        lse = joined(rows_ref[:, half])
        u = -math.log2(N_DST) - lse
        if h == 0 and not copies:
            source_pots_ref[...] = u * (1.0 / SCALE) + src_norm_ref[...]
        pots += [jnp.broadcast_to(u[c : c + 1, :], (8, 128)) for c in range(ROWS // 128)]
    unroll = 4
    for k, (tile_ref, b) in enumerate(tile_blocks(tiles)):

        def rows_of(i, carry, tile_ref=tile_ref, b=b, k=k):
            for g in range(unroll):
                at = pl.ds(pl.multiple_of((i * unroll + g) * 8, 8), 8)
                scores = [tile_ref[b, at, c * 128 : (c + 1) * 128] + pots[c] for c in range(16)]
                high = tree(jnp.maximum, scores)
                total = tree(jnp.add, [jnp.exp2(s - high) for s in scores])
                high_scr[k, at, :] = high
                total_scr[k, at, :] = total
            return carry

        lax.fori_loop(0, COLS // 8 // unroll, rows_of, 0)
    for k, offset in enumerate(OFFSETS):
        at = lax.rem(z + (offset + RING), RING)
        for c in range(COLS // 128):
            rows = slice(c * 128, (c + 1) * 128)
            high = high_scr[k, rows, :]
            top = jnp.max(high, axis=1, keepdims=True)
            total = jnp.sum(total_scr[k, rows, :] * jnp.exp2(high - top), axis=1, keepdims=True)
            lse = as_row(eye, top + log2(total))
            if copies:
                for peer in range(RING):
                    cols_ref[peer, at, c : c + 1, :] = lse
            else:
                cols_ref[at, c : c + 1, :] = lse


def columns(where, rows, src_norm, tiles, copies):
    f32 = jnp.float32
    block = (RING, COLS // 128, 128)
    if copies:
        outs = [jax.ShapeDtypeStruct((RING, *block), f32)]
    else:
        outs = [jax.ShapeDtypeStruct(block, f32), jax.ShapeDtypeStruct((ROWS // 128, 128), f32)]
    return pl.pallas_call(
        functools.partial(columns_kernel, copies),
        out_shape=outs,
        in_specs=[SMEM] + [VMEM] * (2 + len(tiles)),
        out_specs=[VMEM] * len(outs),
        scratch_shapes=[pltpu.VMEM((RING, COLS, 128), f32)] * 2,
        compiler_params=pltpu.CompilerParams(vmem_limit_bytes=28 * MIB),
        cost_estimate=pl.CostEstimate(flops=5 * WIDE * WIDE, bytes_accessed=4 * MIB, transcendentals=WIDE * WIDE),
        name="columns_all" if copies else "columns_own",
    )(where, rows, src_norm, *tiles)


def rows_kernel(where_ref, cols_ref, *refs):
    tiles, (rows_ref, pots_scr, lse_scr) = refs[: len(GROUPS)], refs[len(GROUPS) :]
    z = where_ref[0]
    eye = diagonal()
    for k, offset in enumerate(OFFSETS):
        at = lax.rem(z + (offset + RING), RING)
        w = -math.log2(N_SRC) - joined(cols_ref[:, at])
        for c in range(COLS // 128):
            column = as_column(eye, w[c : c + 1, :])
            pots_scr[2 * k + c] = jnp.broadcast_to(column, (128, 128)).reshape(16, 8, 128)

    def lanes_of(i, carry):
        states = [None, None]
        for k, (tile_ref, b) in enumerate(tile_blocks(tiles)):
            for c in range(COLS // 128):
                pots = pots_scr[2 * k + c]
                for t in range(2):
                    lanes = pl.ds(pl.multiple_of(i * 256 + t * 128, 128), 128)
                    scores = tile_ref[b, c * 128 : (c + 1) * 128, lanes].reshape(16, 8, 128) + pots
                    states[t] = online(scores, states[t])
        lse_scr[i] = jnp.concatenate([over_sublanes(*states[t]) for t in range(2)], axis=0)
        return carry

    lax.fori_loop(0, WIDE // 256, lanes_of, 0)
    put_rows(where_ref, rows_ref, [lse_scr[i, t : t + 1, :] for i in range(WIDE // 256) for t in range(2)])


def rows(where, cols, tiles):
    f32 = jnp.float32
    return pl.pallas_call(
        rows_kernel,
        out_shape=jax.ShapeDtypeStruct((PLANE, 2, ROWS // 128, 128), f32),
        in_specs=[SMEM] + [VMEM] * (1 + len(tiles)),
        out_specs=VMEM,
        scratch_shapes=[pltpu.VMEM((16, 16, 8, 128), f32), pltpu.VMEM((WIDE // 256, 2, 128), f32)],
        compiler_params=pltpu.CompilerParams(vmem_limit_bytes=28 * MIB),
        cost_estimate=pl.CostEstimate(flops=5 * WIDE * WIDE, bytes_accessed=4 * MIB, transcendentals=WIDE * WIDE),
        name="rows_all",
    )(where, cols, *tiles)


def finish_kernel(cols_ref, dst_norm_ref, out_ref):
    w = -math.log2(N_SRC) - joined(cols_ref[...])
    out_ref[...] = w * (1.0 / SCALE) + dst_norm_ref[...]


def shifted(x, axis, by):
    count = lax.axis_size(axis)
    return lax.ppermute(x, axis, [(i, (i + by) % count) for i in range(count)])


def body(sources, targets, duals_init):
    where = jnp.stack([lax.axis_index("z"), lax.axis_index("xl")]).astype(jnp.int32)
    packed = jnp.concatenate([targets, jnp.pad(duals_init.reshape(2, 128), ((0, 6), (0, 0)))], axis=0)
    others = shifted(sources, "xl", 1)
    up, down, ring = [packed], [packed], [packed]
    for step in range(1, RING // 2 + 1):
        up.append(shifted(up[-1], "z", 1))
        ring.append(up[-1])
        if step < RING // 2:
            down.append(shifted(down[-1], "z", -1))
            ring.append(down[-1])
    tiles, at = [], 0
    for g, count in enumerate(GROUPS):
        blocks, at = ring[at : at + count], at + count
        last = g == len(GROUPS) - 1
        if g == 0:
            tile, x, src_norm, dst_norm, *state = build(where, count, blocks, sources=(sources, others))
        else:
            tile, *state = build(where, count, blocks, state=(x, *state), last=last)
        tiles.append(tile)
    row_parts = state[0]
    row_parts = lax.all_to_all(row_parts, PLANE_AXES, 0, 0, tiled=True)
    (col_parts,) = columns(where, row_parts, src_norm, tiles, True)
    col_parts = lax.all_to_all(col_parts, "z", 0, 0, tiled=True)
    row_parts = rows(where, col_parts, tiles)
    row_parts = lax.all_to_all(row_parts, PLANE_AXES, 0, 0, tiled=True)
    col_parts, source_pots = columns(where, row_parts, src_norm, tiles, False)
    col_parts = lax.all_to_all(col_parts, "z", 0, 0, tiled=True)
    target_pots = pl.pallas_call(
        finish_kernel, out_shape=jax.ShapeDtypeStruct((COLS // 128, 128), jnp.float32), name="finish"
    )(col_parts, dst_norm)
    return (source_pots.reshape(ROWS), target_pots.reshape(COLS))


def solution(mesh):
    finer = Mesh(mesh.devices.reshape(2, 8, 4, 2, 2), (*BLK, *TGT))
    return jax.shard_map(
        body,
        mesh=finer,
        in_specs=(P(BLK, None), P((*BLK, *TGT), None), P((*BLK, *TGT))),
        out_specs=(P(BLK), P((*BLK, *TGT))),
        check_vma=False,
    )
```

time: 237 us -> 109 us (0.46)
  other arithmetic: 55.9 us -> 1 us
  blocking collectives: 86.9 us -> 55.4 us
  Pallas kernels: 0 us -> 29.7 us
  waiting for transfers between devices: 36.6 us -> 7.63 us
  matrix products: 17.7 us -> 0 us
  between operations: 14.3 us -> 0.72 us
  local copies, waits for them, and re-layouts: 10 us -> 1.04 us
    reduce_sum x8 -> x0, other arithmetic: 31.6 us -> none  [the longest x2 16.1 us: body(): col_part = jnp.sum(jnp.exp(col_scores - col_high[None, :]), axis=0)]
    pallas_call x0 -> x8, Pallas kernels: none -> 29.7 us  [the longest x2 12.2 us: columns(): pl.pallas_call(functools.partial(columns_kernel, copies), out_shape=outs,...]
    all_gather x1 -> x0, waiting for transfers between devices: 29.2 us -> none  [all_blocks(): blocks = lax.all_gather(blocks, axes[k])]
    all_to_all x6 -> x4, blocking collectives: 80 us -> 55.4 us  [the longest x2 32.9 us: body(): row_parts = lax.all_to_all(row_parts, PLANE_AXES, 0, 0, tiled=True)]
    reduce_max x5 -> x0, other arithmetic: 23.3 us -> none  [the longest x2 15.4 us: body(): col_high = over_copies(jnp.max(col_scores, axis=0), BLK)]
    dot_general x1 -> x0, matrix products: 17.7 us -> none  [cost_of(): jnp.dot(left, right.T, preferred_element_type=jnp.float32, precision=lax....]
    all_to_all x2 -> x0, starting transfers between devices: 14.6 us -> none  [the longest x1 9.13 us: sent_to_all(): lax.all_to_all(jnp.broadcast_to(x[None], (count, *x.shape)), axis, 0, 0,...]
    ppermute x0 -> x8, starting transfers between devices: none -> 13.2 us  [shifted(): return lax.ppermute(x, axis, [(i, (i + by) % count) for i in range(count)])]
  transfers between devices with their start and end apart: 3 -> 8, of which waited for: 2 -> 3; matrix products, arithmetic and copies ran while one was open for 3% -> 1% of each run, Pallas kernels for 0% -> 9%
where the time goes in v1:
time: 109 us
  blocking collectives  55.4 us (51%)
  Pallas kernels  29.7 us (27%)
  starting transfers between devices  13.2 us (12%)
  waiting for transfers between devices  7.63 us (7%)
    all_to_all x2, blocking collectives, body(): row_parts = lax.all_to_all(row_parts, PLANE_AXES, 0, 0, tiled=True)  32.9 us
    all_to_all x2, blocking collectives, body(): col_parts = lax.all_to_all(col_parts, 'z', 0, 0, tiled=True)  22.4 us
    ppermute x8, starting transfers between devices, shifted(): return lax.ppermute(x, axis, [(i, (i + by) % count) for i in range(count)])  13.2 us
    pallas_call x2, Pallas kernels, columns(): pl.pallas_call(functools.partial(columns_kernel, copies), out_shape=outs,...  12.2 us
    pallas_call x4, Pallas kernels, build(): pl.pallas_call(functools.partial(build_kernel, first, last, count), out_s...  11.2 us
    ppermute x8, waiting for transfers between devices, shifted(): return lax.ppermute(x, axis, [(i, (i + by) % count) for i in range(count)])  7.63 us
    pallas_call x1, Pallas kernels, rows(): pl.pallas_call(rows_kernel, out_shape=jax.ShapeDtypeStruct((PLANE, 2, ROW...  4.97 us
  transfers between devices with their start and end apart: 8, of which 3 were waited for; matrix products, arithmetic and copies ran while one was open for 1% of the time, Pallas kernels for 9%

profile of v1, /device:TPU:1, one launch (start us, length us, event | category | flops | bytes accessed | tf_op | source)
XLA Modules:
  0.0 108.7 jit_solution(6437744953310508616)
XLA Ops:
  0.6 2.1 %collective-permute-start = (f32[1024,128]{1,0:T(8,128)}, f32[1024,128]{1,0:T(8,128)S(1)}, u32[]{:S(2)}, u32[]{:S(2)}) collective-permute-start(f32[1024,128]{1,0:T(8,128)} %refs_1_.1), channel_id=1, source_target_pairs={{0,128},{128,0},{1,129},{129,1},{2,130},{130,2},{3,131},{131,3},{4... | collective-permute-start | bytes 1572872 | tf_op jit(solution)/shard_map/ppermute | solution.py:295
  2.7 0.9 select_maximum_fusion.refs_3_
  3.7 1.7 %collective-permute-start.1 = (f32[264,128]{1,0:T(8,128)S(1)}, f32[264,128]{1,0:T(8,128)S(1)}, u32[]{:S(2)}, u32[]{:S(2)}) collective-permute-start(f32[264,128]{1,0:T(8,128)S(1)} %select_maximum_fusion.refs_3_), channel_id=1, source_target_pairs={{0,16},{16,32},{32,48},{48,64},{64,80},{80,96},{96,112},{112,0},{1... | collective-permute-start | bytes 405512 | tf_op jit(solution)/shard_map/ppermute | solution.py:295
  5.4 4.0 %collective-permute-start.2 = (f32[264,128]{1,0:T(8,128)S(1)}, f32[264,128]{1,0:T(8,128)S(1)}, u32[]{:S(2)}, u32[]{:S(2)}) collective-permute-start(f32[264,128]{1,0:T(8,128)S(1)} %select_maximum_fusion.refs_3_), channel_id=1, source_target_pairs={{0,112},{16,0},{32,16},{48,32},{64,48},{80,64},{96,80},{112,96},{1... | collective-permute-start | bytes 405512 | tf_op jit(solution)/shard_map/ppermute | solution.py:295
  9.4 2.9 %collective-permute-done.1.refs_4_ = f32[264,128]{1,0:T(8,128)S(1)} collective-permute-done((f32[264,128]{1,0:T(8,128)S(1)}, f32[264,128]{1,0:T(8,128)S(1)}, u32[]{:S(2)}, u32[]{:S(2)}) %collective-permute-start.1) | collective-permute-done | bytes 135200 | tf_op jit(solution)/shard_map/ppermute | solution.py:295
  12.3 0.0 collective-permute-start.3
  12.3 0.0 collective-permute-done.2.refs_5_
  12.3 2.7 %collective-permute-start.4 = (f32[264,128]{1,0:T(8,128)S(1)}, f32[264,128]{1,0:T(8,128)S(1)}, u32[]{:S(2)}, u32[]{:S(2)}) collective-permute-start(f32[264,128]{1,0:T(8,128)S(1)} %collective-permute-done.2.refs_5_), channel_id=1, source_target_pairs={{0,112},{16,0},{32,16},{48,32},{64,48},{80,64},{96,80},{112,96},{1... | collective-permute-start | bytes 405512 | tf_op jit(solution)/shard_map/ppermute | solution.py:295
  15.0 2.4 %collective-permute-done.3.refs_4_ = f32[264,128]{1,0:T(8,128)S(1)} collective-permute-done((f32[264,128]{1,0:T(8,128)S(1)}, f32[264,128]{1,0:T(8,128)S(1)}, u32[]{:S(2)}, u32[]{:S(2)}) %collective-permute-start.3) | collective-permute-done | bytes 135200 | tf_op jit(solution)/shard_map/ppermute | solution.py:295
  17.4 0.0 collective-permute-start.5
  17.4 0.1 pad_add_fusion.refs_0_.where_ref
  17.5 0.0 collective-permute-done.4.refs_5_
  17.5 2.7 %collective-permute-start.6 = (f32[264,128]{1,0:T(8,128)S(1)}, f32[264,128]{1,0:T(8,128)S(1)}, u32[]{:S(2)}, u32[]{:S(2)}) collective-permute-start(f32[264,128]{1,0:T(8,128)S(1)} %collective-permute-done.4.refs_5_), channel_id=1, source_target_pairs={{0,112},{16,0},{32,16},{48,32},{64,48},{80,64},{96,80},{112,96},{1... | collective-permute-start | bytes 405512 | tf_op jit(solution)/shard_map/ppermute | solution.py:295
  20.2 2.3 %collective-permute-done.5.refs_4_ = f32[264,128]{1,0:T(8,128)S(1)} collective-permute-done((f32[264,128]{1,0:T(8,128)S(1)}, f32[264,128]{1,0:T(8,128)S(1)}, u32[]{:S(2)}, u32[]{:S(2)}) %collective-permute-start.5) | collective-permute-done | bytes 135200 | tf_op jit(solution)/shard_map/ppermute | solution.py:295
  22.5 0.0 collective-permute-start.7
  22.5 0.0 collective-permute-done.refs_2_
  22.5 1.0 copy-done.1
  23.5 3.9 %build_3_10.1 = (f32[3,256,2048]{2,1,0:T(8,128)S(1)}, bf16[2048,768]{1,0:T(8,128)(2,1)S(1)}, f32[8,128]{1,0:T(8,128)S(1)}, f32[2,128]{1,0:T(2,128)S(1)}, f32[8,2048]{1,0:T(8,128)S(1)}, /*index=5*/f32[8,2048]{1,0:T(8,128)S(1)}) custom-call(s32[2]{0:T(128)S(1)} %pad_add_fusion.refs_0_.where_ref, f32[1024,128]{1,0:T(8,128)S(1)} %copy-done.1, ...), custom_call_target="tpu_custom_call" | custom-call | flops 2415919104 | bytes 4194304 | tf_op jit(solution)/shard_map/build_3_10/pallas_call | solution.py:166
  27.4 0.0 copy-start
  27.4 2.7 %build_2_00.2 = (f32[2,256,2048]{2,1,0:T(8,128)S(1)}, f32[8,2048]{1,0:T(8,128)S(1)}, f32[8,2048]{1,0:T(8,128)S(1)}) custom-call(s32[2]{0:T(128)S(1)} %pad_add_fusion.refs_0_.where_ref, bf16[2048,768]{1,0:T(8,128)(2,1)S(1)} %get-tuple-element.18.refs_1_, f32[8,2048]{1,0:T(8,128)S(1)} %get-tuple-element.19.refs_2_, f32[8,2048]{1,0:T(8,128)S(1)} %get-tuple-element.20.refs_3_, ...), custom_call_target="tpu_custom_call" | custom-call | flops 1610612736 | bytes 4194304 | tf_op jit(solution)/shard_map/build_2_00/pallas_call | solution.py:166
  30.2 0.0 collective-permute-done.6.refs_5_
  30.2 2.7 %build_2_00.3 = (f32[2,256,2048]{2,1,0:T(8,128)S(1)}, f32[8,2048]{1,0:T(8,128)S(1)}, f32[8,2048]{1,0:T(8,128)S(1)}) custom-call(s32[2]{0:T(128)S(1)} %pad_add_fusion.refs_0_.where_ref, bf16[2048,768]{1,0:T(8,128)(2,1)S(1)} %get-tuple-element.18.refs_1_, f32[8,2048]{1,0:T(8,128)S(1)} %get-tuple-element.21.refs_2_, f32[8,2048]{1,0:T(8,128)S(1)} %get-tuple-element.22.refs_3_, ...), custom_call_target="tpu_custom_call" | custom-call | flops 1610612736 | bytes 4194304 | tf_op jit(solution)/shard_map/build_2_00/pallas_call | solution.py:166
  32.9 0.0 collective-permute-done.7.refs_4_
  32.9 1.9 %build_1_01.1 = (f32[1,256,2048]{2,1,0:T(8,128)S(1)}, f32[32,2,8,128]{3,2,1,0:T(8,128)S(1)}) custom-call(s32[2]{0:T(128)S(1)} %pad_add_fusion.refs_0_.where_ref, bf16[2048,768]{1,0:T(8,128)(2,1)S(1)} %get-tuple-element.18.refs_1_, f32[8,2048]{1,0:T(8,128)S(1)} %get-tuple-element.23.refs_2_, f32[8,2048]{1,0:T(8,128)S(1)} %get-tuple-element.24.refs_3_, ...), custom_call_target="tpu_custom_call" | custom-call | flops 805306368 | bytes 4194304 | tf_op jit(solution)/shard_map/build_1_01/pallas_call | solution.py:166
  34.8 19.1 %all_to_all.20.rows_ref = f32[32,2,8,128]{3,2,1,0:T(8,128)S(1)} all-to-all(f32[32,2,8,128]{3,2,1,0:T(8,128)S(1)} %get-tuple-element.25), channel_id=1, replica_groups=mesh['xl'=2,'z'=8,'y'=4,'xh'=2,'core'=2] {'xl','y','xh','core'}, dimensions={0} | all-to-all | bytes 524288 | tf_op jit(solution)/shard_map/all_to_all | solution.py:319
  53.9 6.1 %columns_all.1 = f32[8,8,2,128]{3,2,1,0:T(2,128)S(1)} custom-call(s32[2]{0:T(128)S(1)} %pad_add_fusion.refs_0_.where_ref, f32[32,2,8,128]{3,2,1,0:T(8,128)S(1)} %all_to_all.20.rows_ref, f32[8,128]{1,0:T(8,128)S(1)} %get-tuple-element.26.src_norm_ref, f32[3,256,2048]{2,1,0:T(8,128)S(1)} %get-tuple-element.27.refs_0_, ...), custom_call_target="tpu_custom_call" | custom-call | flops 20971520 | bytes 4194304 | tf_op jit(solution)/shard_map/columns_all/pallas_call | solution.py:235
  60.0 12.9 %all_to_all.21.cols_ref = f32[8,8,2,128]{3,2,1,0:T(2,128)S(1)} all-to-all(f32[8,8,2,128]{3,2,1,0:T(2,128)S(1)} %columns_all.1), channel_id=1, replica_groups=mesh['xl'=2,'z'=8,'y'=4,'xh'=2,'core'=2] {'z'}, dimensions={0} | all-to-all | bytes 131072 | tf_op jit(solution)/shard_map/all_to_all | solution.py:321
  72.9 5.0 %rows_all.1 = f32[32,2,8,128]{3,2,1,0:T(8,128)S(1)} custom-call(s32[2]{0:T(128)S(1)} %pad_add_fusion.refs_0_.where_ref, f32[8,8,2,128]{3,2,1,0:T(2,128)S(1)} %all_to_all.21.cols_ref, f32[3,256,2048]{2,1,0:T(8,128)S(1)} %get-tuple-element.27.refs_0_, f32[2,256,2048]{2,1,0:T(8,128)S(1)} %get-tuple-element.28.refs_1_, ...), custom_call_target="tpu_custom_call" | custom-call | flops 20971520 | bytes 4194304 | tf_op jit(solution)/shard_map/rows_all/pallas_call | solution.py:276
  77.9 13.8 %all_to_all.22.rows_ref = f32[32,2,8,128]{3,2,1,0:T(8,128)S(1)} all-to-all(f32[32,2,8,128]{3,2,1,0:T(8,128)S(1)} %rows_all.1), channel_id=1, replica_groups=mesh['xl'=2,'z'=8,'y'=4,'xh'=2,'core'=2] {'xl','y','xh','core'}, dimensions={0} | all-to-all | bytes 524288 | tf_op jit(solution)/shard_map/all_to_all | solution.py:323
  91.7 6.1 %columns_own.1 = (f32[8,2,128]{2,1,0:T(2,128)S(1)}, f32[8,128]{1,0:T(8,128)}) custom-call(s32[2]{0:T(128)S(1)} %pad_add_fusion.refs_0_.where_ref, f32[32,2,8,128]{3,2,1,0:T(8,128)S(1)} %all_to_all.22.rows_ref, f32[8,128]{1,0:T(8,128)S(1)} %get-tuple-element.26.src_norm_ref, f32[3,256,2048]{2,1,0:T(8,128)S(1)} %get-tuple-element.27.refs_0_, ...), custom_call_target="tpu_custom_call" | custom-call | flops 20971520 | bytes 4194304 | tf_op jit(solution)/shard_map/columns_own/pallas_call | solution.py:235
  97.8 9.6 %all_to_all.23.cols_ref = f32[8,2,128]{2,1,0:T(2,128)} all-to-all(f32[8,2,128]{2,1,0:T(2,128)S(1)} %get-tuple-element.32), channel_id=1, replica_groups=mesh['xl'=2,'z'=8,'y'=4,'xh'=2,'core'=2] {'z'}, dimensions={0} | all-to-all | bytes 16384 | tf_op jit(solution)/shard_map/all_to_all | solution.py:325
  107.4 1.3 %finish.1 = f32[2,128]{1,0:T(2,128)} custom-call(f32[8,2,128]{2,1,0:T(2,128)} %all_to_all.23.cols_ref, f32[2,128]{1,0:T(2,128)} %copy-done), custom_call_target="tpu_custom_call" | custom-call | tf_op jit(solution)/shard_map/finish/pallas_call | solution.py:326
  (2 shorter events, 0.0 us)
Async XLA Ops:
  0.6 21.9 %collective-permute-start = (f32[1024,128]{1,0:T(8,128)}, f32[1024,128]{1,0:T(8,128)S(1)}, u32[]{:S(2)}, u32[]{:S(2)}) collective-permute-start(f32[1024,128]{1,0:T(8,128)} %refs_1_.1), channel_id=1, source_target_pairs={{0,128},{128,0},{1,129},{129,1},{2,130},{130,2},{3,131},{131,3},{4... | collective-permute-start | bytes 1572872 | tf_op jit(solution)/shard_map/ppermute | solution.py:295
  3.7 8.7 %collective-permute-start.1 = (f32[264,128]{1,0:T(8,128)S(1)}, f32[264,128]{1,0:T(8,128)S(1)}, u32[]{:S(2)}, u32[]{:S(2)}) collective-permute-start(f32[264,128]{1,0:T(8,128)S(1)} %select_maximum_fusion.refs_3_), channel_id=1, source_target_pairs={{0,16},{16,32},{32,48},{48,64},{64,80},{80,96},{96,112},{112,0},{1... | collective-permute-start | bytes 405512 | tf_op jit(solution)/shard_map/ppermute | solution.py:295
  5.4 7.0 %collective-permute-start.2 = (f32[264,128]{1,0:T(8,128)S(1)}, f32[264,128]{1,0:T(8,128)S(1)}, u32[]{:S(2)}, u32[]{:S(2)}) collective-permute-start(f32[264,128]{1,0:T(8,128)S(1)} %select_maximum_fusion.refs_3_), channel_id=1, source_target_pairs={{0,112},{16,0},{32,16},{48,32},{64,48},{80,64},{96,80},{112,96},{1... | collective-permute-start | bytes 405512 | tf_op jit(solution)/shard_map/ppermute | solution.py:295
  12.3 5.1 %collective-permute-start.3 = (f32[264,128]{1,0:T(8,128)S(1)}, f32[264,128]{1,0:T(8,128)S(1)}, u32[]{:S(2)}, u32[]{:S(2)}) collective-permute-start(f32[264,128]{1,0:T(8,128)S(1)} %collective-permute-done.1.refs_4_), channel_id=1, source_target_pairs={{0,16},{16,32},{32,48},{48,64},{64,80},{80,96},{96,112},{112,0},{1... | collective-permute-start | bytes 405512 | tf_op jit(solution)/shard_map/ppermute | solution.py:295
  12.3 5.1 %collective-permute-start.4 = (f32[264,128]{1,0:T(8,128)S(1)}, f32[264,128]{1,0:T(8,128)S(1)}, u32[]{:S(2)}, u32[]{:S(2)}) collective-permute-start(f32[264,128]{1,0:T(8,128)S(1)} %collective-permute-done.2.refs_5_), channel_id=1, source_target_pairs={{0,112},{16,0},{32,16},{48,32},{64,48},{80,64},{96,80},{112,96},{1... | collective-permute-start | bytes 405512 | tf_op jit(solution)/shard_map/ppermute | solution.py:295
  17.4 5.1 %collective-permute-start.5 = (f32[264,128]{1,0:T(8,128)S(1)}, f32[264,128]{1,0:T(8,128)S(1)}, u32[]{:S(2)}, u32[]{:S(2)}) collective-permute-start(f32[264,128]{1,0:T(8,128)S(1)} %collective-permute-done.3.refs_4_), channel_id=1, source_target_pairs={{0,16},{16,32},{32,48},{48,64},{64,80},{80,96},{96,112},{112,0},{1... | collective-permute-start | bytes 405512 | tf_op jit(solution)/shard_map/ppermute | solution.py:295
  17.5 12.7 %collective-permute-start.6 = (f32[264,128]{1,0:T(8,128)S(1)}, f32[264,128]{1,0:T(8,128)S(1)}, u32[]{:S(2)}, u32[]{:S(2)}) collective-permute-start(f32[264,128]{1,0:T(8,128)S(1)} %collective-permute-done.4.refs_5_), channel_id=1, source_target_pairs={{0,112},{16,0},{32,16},{48,32},{64,48},{80,64},{96,80},{112,96},{1... | collective-permute-start | bytes 405512 | tf_op jit(solution)/shard_map/ppermute | solution.py:295
  22.5 10.4 %collective-permute-start.7 = (f32[264,128]{1,0:T(8,128)S(1)}, f32[264,128]{1,0:T(8,128)S(1)}, u32[]{:S(2)}, u32[]{:S(2)}) collective-permute-start(f32[264,128]{1,0:T(8,128)S(1)} %collective-permute-done.5.refs_4_), channel_id=1, source_target_pairs={{0,16},{16,32},{32,48},{48,64},{64,80},{80,96},{96,112},{112,0},{1... | collective-permute-start | bytes 405512 | tf_op jit(solution)/shard_map/ppermute | solution.py:295
  22.5 1.0 copy-start.1
  27.4 5.5 %copy-start = (f32[2,128]{1,0:T(2,128)}, f32[2,128]{1,0:T(2,128)S(1)}, u32[]{:S(2)}) copy-start(f32[2,128]{1,0:T(2,128)S(1)} %get-tuple-element.33.dst_norm_ref) | copy-start | bytes 3076

commit v2 on v0

v2 whole, which is shorter than its diff:
```python
import functools
import math

import jax
import jax.numpy as jnp
from jax import lax
from jax.experimental import pallas as pl
from jax.experimental.pallas import tpu as pltpu
from jax.sharding import Mesh
from jax.sharding import PartitionSpec as P


EPS = 0.05
SCALE = math.log2(math.e) / EPS
LOG2E = math.log2(math.e)
N_SRC = 16384
N_DST = 65536
ROWS = 1024
COLS = 256
RING = 8
PLANE = 16
LANES = 128
TILES = ROWS // LANES
MIB = 1024 * 1024

BLK = ("xl", "z")
TGT = ("y", "xh", "core")
PLANE_AXES = ("xl", "y", "xh")

VMEM = pl.BlockSpec(memory_space=pltpu.VMEM)


def log2(x):
    return jnp.log(x) * LOG2E


def diagonal():
    shape = (LANES, LANES)
    return lax.broadcasted_iota(jnp.int32, shape, 0) == lax.broadcasted_iota(jnp.int32, shape, 1)


def as_column(eye, row):
    return jnp.sum(jnp.where(eye, row, 0.0), axis=1, keepdims=True)


def as_row(eye, column):
    return jnp.sum(jnp.where(eye, column, 0.0), axis=0, keepdims=True)


def tree(op, parts):
    parts = list(parts)
    while len(parts) > 1:
        parts = [op(*parts[k : k + 2]) if k + 1 < len(parts) else parts[k] for k in range(0, len(parts), 2)]
    return parts[0]


def three_parts(x):
    high = x.astype(jnp.bfloat16)
    rest = x - high.astype(jnp.float32)
    mid = rest.astype(jnp.bfloat16)
    low = (rest - mid.astype(jnp.float32)).astype(jnp.bfloat16)
    return high, mid, low


def online(scores, state):
    high = tree(jnp.maximum, scores)
    if state is None:
        return high, tree(jnp.add, [jnp.exp2(s - high) for s in scores])
    high = jnp.maximum(high, state[0])
    total = tree(jnp.add, [jnp.exp2(s - high) for s in scores])
    return high, state[1] * jnp.exp2(state[0] - high) + total


def over_sublanes(high, total):
    top = jnp.max(high, axis=0, keepdims=True)
    return top + log2(jnp.sum(total * jnp.exp2(high - top), axis=0, keepdims=True))


def joined(parts):
    top = jnp.max(parts, axis=0)
    return top + log2(jnp.sum(jnp.exp2(parts - top[None]), axis=0))


def put_rows(rows_ref, state_of):
    for half in range(2):
        tiles = [slice(t * LANES, (t + 1) * LANES) for t in range(TILES)]
        lse = jnp.concatenate([over_sublanes(*state_of(half, tile)) for tile in tiles], axis=0)
        for peer in range(PLANE):
            rows_ref[peer, half] = lse


def prepare_sources(x, half, x_ref):
    turned = (x * (2.0 * SCALE)).T
    high, mid, low = three_parts(turned)
    for k, part in enumerate((high, high, mid, mid, low, high)):
        x_ref[half, k * LANES : (k + 1) * LANES, :] = part


def prepare_targets(eye, block_ref, pots_ref):
    y = block_ref[0:COLS, :]
    norms = jnp.sum(y * y, axis=1, keepdims=True)
    for c in range(COLS // LANES):
        rows = slice(c * LANES, (c + 1) * LANES)
        column = as_column(eye, block_ref[COLS + c : COLS + c + 1, :])
        pots_ref[rows, :] = jnp.broadcast_to((column - norms[rows]) * SCALE, (LANES, LANES))
    high, mid, low = three_parts(y)
    return jnp.concatenate([high, mid, high, mid, high, low], axis=1), norms


def add_block(parts, pots_ref, at, half, x_ref, tile_ref, state_ref, fresh):
    step = 512
    for n in range(ROWS // step):
        lanes = slice(n * step, (n + 1) * step)
        tile_ref[at, half, :, lanes] = jnp.dot(parts, x_ref[half, :, lanes], preferred_element_type=jnp.float32)
        for t in range(n * step // LANES, (n + 1) * step // LANES):
            tile = slice(t * LANES, (t + 1) * LANES)
            state = None if fresh else (state_ref[0, half, :, tile], state_ref[1, half, :, tile])
            for c in range(2):
                rows = range(c * LANES, (c + 1) * LANES, 8)
                state = online([tile_ref[at, half, r : r + 8, tile] + pots_ref[r : r + 8, :] for r in rows], state)
            state_ref[0, half, :, tile], state_ref[1, half, :, tile] = state


def start_kernel(sources_ref, block_ref, tile_ref, x_ref, state_ref, src_norm_ref, dst_norm_ref, pots_scr):
    z, mine = lax.axis_index("z"), lax.axis_index("xl")
    eye = diagonal()
    x = sources_ref[...]
    prepare_sources(x, mine, x_ref)
    squares = jnp.sum(x * x, axis=1, keepdims=True)
    for c in range(TILES):
        src_norm_ref[c : c + 1, :] = as_row(eye, squares[c * LANES : (c + 1) * LANES])
    parts, norms = prepare_targets(eye, block_ref, pots_scr)
    for c in range(COLS // LANES):
        dst_norm_ref[c : c + 1, :] = as_row(eye, norms[c * LANES : (c + 1) * LANES])
    add_block(parts, pots_scr, z, mine, x_ref, tile_ref, state_ref, True)


def second_kernel(sources_ref, own_ref, lower_ref, upper_ref, *refs):
    (tile_ref, x_ref, state_ref), pots_scr = refs[3:6], refs[6]
    z, mine = lax.axis_index("z"), lax.axis_index("xl")
    eye = diagonal()
    prepare_sources(sources_ref[...], 1 - mine, x_ref)
    for b, (block_ref, offset) in enumerate(((own_ref, 0), (lower_ref, -1), (upper_ref, 1))):
        parts, _ = prepare_targets(eye, block_ref, pots_scr.at[b])
        at = lax.rem(z + (offset + RING), RING)
        if offset:
            add_block(parts, pots_scr.at[b], at, mine, x_ref, tile_ref, state_ref, False)
        add_block(parts, pots_scr.at[b], at, 1 - mine, x_ref, tile_ref, state_ref, not offset)


def more_kernel(offsets, last, x_ref, *refs):
    count = len(offsets)
    blocks, (tile_ref, state_ref) = refs[:count], refs[count + 2 : count + 4]
    pots_scr = refs[-1]
    z = lax.axis_index("z")
    eye = diagonal()
    for b, offset in enumerate(offsets):
        parts, _ = prepare_targets(eye, blocks[b], pots_scr.at[b])
        at = lax.rem(z + (offset + RING), RING)
        for half in range(2):
            add_block(parts, pots_scr.at[b], at, half, x_ref, tile_ref, state_ref, False)
    if last:
        put_rows(refs[count + 4], lambda half, tile: (state_ref[0, half, :, tile], state_ref[1, half, :, tile]))


F32 = jnp.float32
TILE = jax.ShapeDtypeStruct((RING, 2, COLS, ROWS), F32)
PARTS = jax.ShapeDtypeStruct((2, 6 * LANES, ROWS), jnp.bfloat16)
STATE = jax.ShapeDtypeStruct((2, 2, 8, ROWS), F32)
ROW_LSE = jax.ShapeDtypeStruct((PLANE, 2, TILES, LANES), F32)


def call(kernel, args, outs, blocks, scratch=(), aliases={}):
    return pl.pallas_call(
        kernel,
        out_shape=outs,
        in_specs=[VMEM] * len(args),
        out_specs=[VMEM] * len(outs),
        scratch_shapes=list(scratch),
        input_output_aliases=aliases,
        compiler_params=pltpu.CompilerParams(vmem_limit_bytes=24 * MIB),
        cost_estimate=pl.CostEstimate(
            flops=blocks * 2 * COLS * ROWS * 768, bytes_accessed=MIB, transcendentals=blocks * COLS * ROWS
        ),
    )(*args)


def columns_kernel(copies, rows_ref, src_norm_ref, tile_ref, *refs):
    if copies:
        cols_ref, high_scr, total_scr, lse_scr = refs
    else:
        cols_ref, source_pots_ref, high_scr, total_scr, lse_scr = refs
    u = -math.log2(N_DST) - joined(rows_ref[...])
    if not copies:
        mine = lax.axis_index("xl")
        own = jnp.where(mine == 0, u[0], u[1])
        source_pots_ref[...] = own * (1.0 / SCALE) + src_norm_ref[...]
    pots = [jnp.broadcast_to(u[h, t : t + 1, :], (8, LANES)) for h in range(2) for t in range(TILES)]
    high_scr[...] = jnp.zeros_like(high_scr)
    total_scr[...] = jnp.ones_like(total_scr)

    def finish(k):
        for c in range(COLS // LANES):
            rows = slice(c * LANES, (c + 1) * LANES)
            high, total = high_scr[rows, :].T, total_scr[rows, :].T
            top = jnp.max(high, axis=0, keepdims=True)
            lse_scr[k, c : c + 1, :] = top + log2(jnp.sum(total * jnp.exp2(high - top), axis=0, keepdims=True))

    def block(k, carry):
        finish(jnp.maximum(k - 1, 0))
        for r in range(0, COLS, 8):
            scores = [
                tile_ref[k, h, r : r + 8, t * LANES : (t + 1) * LANES] + pots[h * TILES + t]
                for h in range(2)
                for t in range(TILES)
            ]
            high_scr[r : r + 8, :], total_scr[r : r + 8, :] = online(scores, None)
        return carry

    lax.fori_loop(0, RING, block, 0)
    finish(RING - 1)
    if copies:
        lse = lse_scr[...].reshape(RING * 2, LANES)
        for peer in range(RING):
            cols_ref[peer] = lse
    else:
        cols_ref[...] = lse_scr[...]


def columns(rows, src_norm, tile, copies):
    if copies:
        outs = [jax.ShapeDtypeStruct((RING, RING * 2, LANES), F32)]
    else:
        outs = [jax.ShapeDtypeStruct((RING, 2, LANES), F32), jax.ShapeDtypeStruct((TILES, LANES), F32)]
    scratch = [pltpu.VMEM((COLS, LANES), F32)] * 2 + [pltpu.VMEM((RING, 2, LANES), F32)]
    return call(functools.partial(columns_kernel, copies), (rows, src_norm, tile), outs, 16, scratch)


def rows_kernel(cols_ref, tile_ref, rows_ref, w_scr, pots_scr, high_scr, total_scr):
    eye = diagonal()
    w_scr[...] = (-math.log2(N_SRC) - joined(cols_ref[...])).reshape(RING, 2, LANES)
    high_scr[...] = jnp.full_like(high_scr, -3.0e38)
    total_scr[...] = jnp.zeros_like(total_scr)

    def spread(k, slot):
        for c in range(2):
            column = as_column(eye, w_scr[k, c : c + 1, :])
            pots_scr[slot, c * LANES : (c + 1) * LANES, :] = jnp.broadcast_to(column, (LANES, LANES))

    def block(k, slot):
        for half in range(2):
            for t in range(TILES):
                tile = slice(t * LANES, (t + 1) * LANES)
                state = high_scr[half, :, tile], total_scr[half, :, tile]
                for c in range(2):
                    rows = range(c * LANES, (c + 1) * LANES, 8)
                    scores = [tile_ref[k, half, r : r + 8, tile] + pots_scr[slot, r : r + 8, :] for r in rows]
                    state = online(scores, state)
                high_scr[half, :, tile], total_scr[half, :, tile] = state

    def two_blocks(i, carry):
        spread(2 * i + 1, 1)
        block(2 * i, 0)
        spread(jnp.minimum(2 * i + 2, RING - 1), 0)
        block(2 * i + 1, 1)
        return carry

    spread(0, 0)
    lax.fori_loop(0, RING // 2, two_blocks, 0)
    put_rows(rows_ref, lambda half, tile: (high_scr[half, :, tile], total_scr[half, :, tile]))


def rows(cols, tile):
    scratch = [
        pltpu.VMEM((RING, 2, LANES), F32),
        pltpu.VMEM((2, COLS, LANES), F32),
        pltpu.VMEM((2, 8, ROWS), F32),
        pltpu.VMEM((2, 8, ROWS), F32),
    ]
    return call(rows_kernel, (cols, tile), [ROW_LSE], 16, scratch)[0]


def shifted(x, axis, by):
    count = lax.axis_size(axis)
    return lax.ppermute(x, axis, [(i, (i + by) % count) for i in range(count)])


def over_plane(copies):
    return lax.all_gather(lax.all_to_all(copies, PLANE_AXES, 0, 0, tiled=True), "core", tiled=True)


def steps(sources, targets, duals_init):
    packed = jnp.concatenate([targets, jnp.pad(duals_init.reshape(2, LANES), ((0, 6), (0, 0)))], axis=0)
    others = shifted(sources, "xl", 1)
    up, down = [packed], [packed]
    for step in range(1, RING // 2 + 1):
        up.append(shifted(up[-1], "z", 1))
        if step < RING // 2:
            down.append(shifted(down[-1], "z", -1))
    pots = pltpu.VMEM((COLS, LANES), F32)
    norms = [jax.ShapeDtypeStruct((TILES, LANES), F32), jax.ShapeDtypeStruct((2, LANES), F32)]
    tile, x, state, src_norm, dst_norm = call(start_kernel, (sources, packed), [TILE, PARTS, STATE, *norms], 1, [pots])
    tile, x, state = call(
        second_kernel,
        (others, packed, up[1], down[1], tile, x, state),
        [TILE, PARTS, STATE],
        5,
        [pltpu.VMEM((3, COLS, LANES), F32)],
        {4: 0, 5: 1, 6: 2},
    )
    for step in (2, 3, 4):
        last = step == RING // 2
        blocks = (up[step],) if last else (up[step], down[step])
        offsets = (-step,) if last else (-step, step)
        tile, state, *row_lse = call(
            functools.partial(more_kernel, offsets, last),
            (x, *blocks, tile, state),
            [TILE, STATE] + [ROW_LSE] * last,
            2 * len(blocks),
            [pltpu.VMEM((2, COLS, LANES), F32)],
            {1 + len(blocks): 0, 2 + len(blocks): 1},
        )
    (col_lse,) = columns(over_plane(row_lse[0]), src_norm, tile, True)
    row_lse = rows(lax.all_to_all(col_lse, "z", 0, 0, tiled=True), tile)
    col_lse, source_pots = columns(over_plane(row_lse), src_norm, tile, False)
    col_lse = joined(lax.all_to_all(col_lse, "z", 0, 0, tiled=True))
    target_pots = (-math.log2(N_SRC) - col_lse) * (1.0 / SCALE) + dst_norm
    return (source_pots.reshape(ROWS), target_pots.reshape(COLS))


def solution(mesh):
    finer = Mesh(mesh.devices.reshape(2, 8, 4, 2, 2), (*BLK, *TGT))
    return jax.shard_map(
        steps,
        mesh=finer,
        in_specs=(P(BLK, None), P((*BLK, *TGT), None), P((*BLK, *TGT))),
        out_specs=(P(BLK), P((*BLK, *TGT))),
        check_vma=False,
    )
```

time: 237 us -> 101 us (0.43)
  other arithmetic: 55.9 us -> 1.56 us
  waiting for transfers between devices: 36.6 us -> 5.75 us
  blocking collectives: 86.9 us -> 56.5 us
  Pallas kernels: 0 us -> 21.6 us
  matrix products: 17.7 us -> 0 us
  between operations: 14.3 us -> 0.71 us
  local copies, waits for them, and re-layouts: 10 us -> 1.04 us
    all_to_all x6 -> x4, blocking collectives: 80 us -> 44.7 us  [the longest x2 22.9 us: over_plane(): lax.all_to_all(copies, PLANE_AXES, 0, 0, tiled=True)]
    reduce_sum x8 -> x1, other arithmetic: 31.6 us -> 0.03 us  [joined(): return top + log2(jnp.sum(jnp.exp2(parts - top[None]), axis=0))]
    all_gather x1 -> x0, waiting for transfers between devices: 29.2 us -> none  [all_blocks(): blocks = lax.all_gather(blocks, axes[k])]
    reduce_max x5 -> x1, other arithmetic: 23.3 us -> 0.02 us  [joined(): top = jnp.max(parts, axis=0)]
    pallas_call x0 -> x8, Pallas kernels: none -> 21.6 us  [call(): pl.pallas_call(kernel, out_shape=outs, in_specs=[VMEM] * len(args), out_s...]
    dot_general x1 -> x0, matrix products: 17.7 us -> none  [cost_of(): jnp.dot(left, right.T, preferred_element_type=jnp.float32, precision=lax....]
    all_to_all x2 -> x0, starting transfers between devices: 14.6 us -> none  [the longest x1 9.13 us: sent_to_all(): lax.all_to_all(jnp.broadcast_to(x[None], (count, *x.shape)), axis, 0, 0,...]
    ppermute x0 -> x8, starting transfers between devices: none -> 13.3 us  [shifted(): return lax.ppermute(x, axis, [(i, (i + by) % count) for i in range(count)])]
  transfers between devices with their start and end apart: 3 -> 8, of which waited for: 2 -> 3; matrix products, arithmetic and copies ran while one was open for 3% -> 1% of each run, Pallas kernels for 0% -> 8%
where the time goes in v2:
time: 101 us; the launch traced here: 100 us
  blocking collectives  56.5 us (56%)
  Pallas kernels  21.6 us (21%)
  starting transfers between devices  13.3 us (13%)
  waiting for transfers between devices  5.75 us (6%)
  other arithmetic  1.56 us (2%)
  local copies, waits for them, and re-layouts  1.04 us (1%)
    all_to_all x2, blocking collectives, over_plane(): lax.all_to_all(copies, PLANE_AXES, 0, 0, tiled=True)  22.9 us
    pallas_call x8, Pallas kernels, call(): pl.pallas_call(kernel, out_shape=outs, in_specs=[VMEM] * len(args), out_s...  21.6 us
    ppermute x8, starting transfers between devices, shifted(): return lax.ppermute(x, axis, [(i, (i + by) % count) for i in range(count)])  13.3 us
    all_to_all x1, blocking collectives, steps(): row_lse = rows(lax.all_to_all(col_lse, 'z', 0, 0, tiled=True), tile)  12.9 us
    all_gather x2, blocking collectives, over_plane(): lax.all_gather(lax.all_to_all(copies, PLANE_AXES, 0, 0, tiled=True), 'cor...  11.7 us
    all_to_all x1, blocking collectives, steps(): col_lse = joined(lax.all_to_all(col_lse, 'z', 0, 0, tiled=True))  8.94 us
    ppermute x8, waiting for transfers between devices, shifted(): return lax.ppermute(x, axis, [(i, (i + by) % count) for i in range(count)])  5.75 us
  transfers between devices with their start and end apart: 8, of which 3 were waited for; matrix products, arithmetic and copies ran while one was open for 1% of the time, Pallas kernels for 8%

profile of v2, /device:TPU:1, one launch (start us, length us, event | category | flops | bytes accessed | tf_op | source)
XLA Modules:
  0.0 100.4 jit_solution(4641918902374613825)
XLA Ops:
  0.6 2.1 %collective-permute-start = (f32[1024,128]{1,0:T(8,128)}, f32[1024,128]{1,0:T(8,128)S(1)}, u32[]{:S(2)}, u32[]{:S(2)}) collective-permute-start(f32[1024,128]{1,0:T(8,128)} %sources_ref.1), channel_id=1, source_target_pairs={{0,128},{128,0},{1,129},{129,1},{2,130},{130,2},{3,131},{131,3},{4... | collective-permute-start | bytes 1572872 | tf_op jit(solution)/shard_map/ppermute | solution.py:285
  2.7 0.9 select_maximum_fusion.block_ref.own_ref
  3.7 1.7 %collective-permute-start.1 = (f32[264,128]{1,0:T(8,128)S(1)}, f32[264,128]{1,0:T(8,128)S(1)}, u32[]{:S(2)}, u32[]{:S(2)}) collective-permute-start(f32[264,128]{1,0:T(8,128)S(1)} %select_maximum_fusion.block_ref.own_ref), channel_id=1, source_target_pairs={{0,16},{16,32},{32,48},{48,64},{64,80},{80,96},{96,112},{112,0},{1... | collective-permute-start | bytes 405512 | tf_op jit(solution)/shard_map/ppermute | solution.py:285
  5.4 4.0 %collective-permute-start.2 = (f32[264,128]{1,0:T(8,128)S(1)}, f32[264,128]{1,0:T(8,128)S(1)}, u32[]{:S(2)}, u32[]{:S(2)}) collective-permute-start(f32[264,128]{1,0:T(8,128)S(1)} %select_maximum_fusion.block_ref.own_ref), channel_id=1, source_target_pairs={{0,112},{16,0},{32,16},{48,32},{64,48},{80,64},{96,80},{112,96},{1... | collective-permute-start | bytes 405512 | tf_op jit(solution)/shard_map/ppermute | solution.py:285
  9.4 2.9 %collective-permute-done.1.lower_ref = f32[264,128]{1,0:T(8,128)S(1)} collective-permute-done((f32[264,128]{1,0:T(8,128)S(1)}, f32[264,128]{1,0:T(8,128)S(1)}, u32[]{:S(2)}, u32[]{:S(2)}) %collective-permute-start.1) | collective-permute-done | bytes 135200 | tf_op jit(solution)/shard_map/ppermute | solution.py:285
  12.3 0.0 collective-permute-start.3
  12.3 0.0 collective-permute-done.2.upper_ref
  12.3 2.7 %collective-permute-start.6 = (f32[264,128]{1,0:T(8,128)S(1)}, f32[264,128]{1,0:T(8,128)S(1)}, u32[]{:S(2)}, u32[]{:S(2)}) collective-permute-start(f32[264,128]{1,0:T(8,128)S(1)} %collective-permute-done.2.upper_ref), channel_id=1, source_target_pairs={{0,112},{16,0},{32,16},{48,32},{64,48},{80,64},{96,80},{112,96},{1... | collective-permute-start | bytes 405512 | tf_op jit(solution)/shard_map/ppermute | solution.py:285
  15.0 2.4 %collective-permute-done.3.refs_0_ = f32[264,128]{1,0:T(8,128)S(1)} collective-permute-done((f32[264,128]{1,0:T(8,128)S(1)}, f32[264,128]{1,0:T(8,128)S(1)}, u32[]{:S(2)}, u32[]{:S(2)}) %collective-permute-start.3) | collective-permute-done | bytes 135200 | tf_op jit(solution)/shard_map/ppermute | solution.py:285
  17.4 0.0 collective-permute-start.4
  17.4 1.0 %copy-done = f32[1024,128]{1,0:T(8,128)S(1)} copy-done((f32[1024,128]{1,0:T(8,128)S(1)}, f32[1024,128]{1,0:T(8,128)}, u32[]{:S(2)}) %copy-start) | copy-done | bytes 524312
  18.5 0.8 shard_map.50
  19.3 0.0 collective-permute-done.6.refs_1_
  19.3 2.7 %collective-permute-start.7 = (f32[264,128]{1,0:T(8,128)S(1)}, f32[264,128]{1,0:T(8,128)S(1)}, u32[]{:S(2)}, u32[]{:S(2)}) collective-permute-start(f32[264,128]{1,0:T(8,128)S(1)} %collective-permute-done.6.refs_1_), channel_id=1, source_target_pairs={{0,112},{16,0},{32,16},{48,32},{64,48},{80,64},{96,80},{112,96},{1... | collective-permute-start | bytes 405512 | tf_op jit(solution)/shard_map/ppermute | solution.py:285
  22.1 0.4 collective-permute-done.4.refs_0_
  22.5 0.0 collective-permute-start.5
  22.5 0.0 collective-permute-done.sources_ref
  22.5 2.8 %shard_map.51 = (f32[8,2,256,1024]{3,2,1,0:T(8,128)S(1)}, bf16[2,768,1024]{2,1,0:T(8,128)(2,1)S(1)}, f32[2,2,8,1024]{3,2,1,0:T(8,128)S(1)}) custom-call(f32[1024,128]{1,0:T(8,128)S(1)} %collective-permute-done.sources_ref, f32[264,128]{1,0:T(8,128)S(1)} %select_maximum_fusion.block_ref.own_ref, ...), custom_call_target="tpu_custom_call", output_to_operand_aliasing={{0}: (4, {}), {1}: (5, {}), {2}: (6, {})} | custom-call | flops 2013265920 | bytes 1048576 | tf_op jit(solution)/shard_map/pallas_call | solution.py:174
  25.3 2.2 %shard_map.52 = (f32[8,2,256,1024]{3,2,1,0:T(8,128)S(1)}, f32[2,2,8,1024]{3,2,1,0:T(8,128)S(1)}) custom-call(bf16[2,768,1024]{2,1,0:T(8,128)(2,1)S(1)} %get-tuple-element.21.x_ref, f32[264,128]{1,0:T(8,128)S(1)} %collective-permute-done.3.refs_0_, f32[264,128]{1,0:T(8,128)S(1)} %collective-permute-done.6.refs_1_, ...), custom_call_target="tpu_custom_call", output_to_operand_aliasing={{0}: (3, {}), {1}: (4, {})} | custom-call | flops 1610612736 | bytes 1048576 | tf_op jit(solution)/shard_map/pallas_call | solution.py:174
  27.5 0.0 collective-permute-done.7.refs_1_
  27.5 2.2 %shard_map.53 = (f32[8,2,256,1024]{3,2,1,0:T(8,128)S(1)}, f32[2,2,8,1024]{3,2,1,0:T(8,128)S(1)}) custom-call(bf16[2,768,1024]{2,1,0:T(8,128)(2,1)S(1)} %get-tuple-element.21.x_ref, f32[264,128]{1,0:T(8,128)S(1)} %collective-permute-done.4.refs_0_, f32[264,128]{1,0:T(8,128)S(1)} %collective-permute-done.7.refs_1_, ...), custom_call_target="tpu_custom_call", output_to_operand_aliasing={{0}: (3, {}), {1}: (4, {})} | custom-call | flops 1610612736 | bytes 1048576 | tf_op jit(solution)/shard_map/pallas_call | solution.py:174
  29.8 1.3 %shard_map.54 = (f32[8,2,256,1024]{3,2,1,0:T(8,128)S(1)}, f32[2,2,8,1024]{3,2,1,0:T(8,128)S(1)}, f32[16,2,8,128]{3,2,1,0:T(8,128)S(1)}) custom-call(bf16[2,768,1024]{2,1,0:T(8,128)(2,1)S(1)} %get-tuple-element.21.x_ref, f32[264,128]{1,0:T(8,128)S(1)} %collective-permute-done.5.refs_0_, ...), custom_call_target="tpu_custom_call", output_to_operand_aliasing={{0}: (2, {}), {1}: (3, {})} | custom-call | flops 805306368 | bytes 1048576 | tf_op jit(solution)/shard_map/pallas_call | solution.py:174
  31.0 13.2 %all_to_all.20 = f32[16,2,8,128]{3,2,1,0:T(8,128)S(1)} all-to-all(f32[16,2,8,128]{3,2,1,0:T(8,128)S(1)} %get-tuple-element.28), channel_id=1, replica_groups=mesh['xl'=2,'z'=8,'y'=4,'xh'=2,'core'=2] {'xl','y','xh'}, dimensions={0} | all-to-all | bytes 262144 | tf_op jit(solution)/shard_map/all_to_all | solution.py:289
  44.2 6.9 %all_gather.6.rows_ref = f32[32,2,8,128]{3,2,1,0:T(8,128)S(1)} all-gather(f32[16,2,8,128]{3,2,1,0:T(8,128)S(1)} %all_to_all.20), channel_id=1, replica_groups=mesh['xl'=2,'z'=8,'y'=4,'xh'=2,'core'=2] {'core'}, dimensions={0}, use_global_device_ids=true | all-gather | bytes 393216 | tf_op jit(solution)/shard_map/all_gather | solution.py:289
  51.1 4.1 %shard_map.55 = f32[8,16,128]{2,1,0:T(8,128)S(1)} custom-call(f32[32,2,8,128]{3,2,1,0:T(8,128)S(1)} %all_gather.6.rows_ref, f32[8,128]{1,0:T(8,128)S(1)} %get-tuple-element.29.src_norm_ref, f32[8,2,256,1024]{3,2,1,0:T(8,128)S(1)} %get-tuple-element.30.tile_ref), custom_call_target="tpu_custom_call" | custom-call | flops 6442450944 | bytes 1048576 | tf_op jit(solution)/shard_map/pallas_call | solution.py:174
  55.2 12.9 %all_to_all.21.cols_ref = f32[8,16,128]{2,1,0:T(8,128)S(1)} all-to-all(f32[8,16,128]{2,1,0:T(8,128)S(1)} %shard_map.55), channel_id=1, replica_groups=mesh['xl'=2,'z'=8,'y'=4,'xh'=2,'core'=2] {'z'}, dimensions={0} | all-to-all | bytes 131072 | tf_op jit(solution)/shard_map/all_to_all | solution.py:324
  68.1 4.0 %shard_map.56 = f32[16,2,8,128]{3,2,1,0:T(8,128)S(1)} custom-call(f32[8,16,128]{2,1,0:T(8,128)S(1)} %all_to_all.21.cols_ref, f32[8,2,256,1024]{3,2,1,0:T(8,128)S(1)} %get-tuple-element.30.tile_ref), custom_call_target="tpu_custom_call" | custom-call | flops 6442450944 | bytes 1048576 | tf_op jit(solution)/shard_map/pallas_call | solution.py:174
  72.1 9.7 %all_to_all.22 = f32[16,2,8,128]{3,2,1,0:T(8,128)S(1)} all-to-all(f32[16,2,8,128]{3,2,1,0:T(8,128)S(1)} %shard_map.56), channel_id=1, replica_groups=mesh['xl'=2,'z'=8,'y'=4,'xh'=2,'core'=2] {'xl','y','xh'}, dimensions={0} | all-to-all | bytes 262144 | tf_op jit(solution)/shard_map/all_to_all | solution.py:289
  81.8 4.8 %all_gather.7.rows_ref = f32[32,2,8,128]{3,2,1,0:T(8,128)S(1)} all-gather(f32[16,2,8,128]{3,2,1,0:T(8,128)S(1)} %all_to_all.22), channel_id=1, replica_groups=mesh['xl'=2,'z'=8,'y'=4,'xh'=2,'core'=2] {'core'}, dimensions={0}, use_global_device_ids=true | all-gather | bytes 393216 | tf_op jit(solution)/shard_map/all_gather | solution.py:289
  86.7 4.1 %shard_map.57 = (f32[8,2,128]{2,1,0:T(2,128)S(1)}, f32[8,128]{1,0:T(8,128)}) custom-call(f32[32,2,8,128]{3,2,1,0:T(8,128)S(1)} %all_gather.7.rows_ref, f32[8,128]{1,0:T(8,128)S(1)} %get-tuple-element.29.src_norm_ref, f32[8,2,256,1024]{3,2,1,0:T(8,128)S(1)} %get-tuple-element.30.tile_ref), custom_call_target="tpu_custom_call" | custom-call | flops 6442450944 | bytes 1048576 | tf_op jit(solution)/shard_map/pallas_call | solution.py:174
  90.8 8.9 %all_to_all.23 = f32[8,2,128]{2,1,0:T(2,128)S(1)} all-to-all(f32[8,2,128]{2,1,0:T(2,128)S(1)} %get-tuple-element.32), channel_id=1, replica_groups=mesh['xl'=2,'z'=8,'y'=4,'xh'=2,'core'=2] {'z'}, dimensions={0} | all-to-all | bytes 16384 | tf_op jit(solution)/shard_map/all_to_all | solution.py:326
  99.8 0.6 add_bitcast_fusion
  (4 shorter events, 0.1 us)
Async XLA Ops:
  0.6 21.9 %collective-permute-start = (f32[1024,128]{1,0:T(8,128)}, f32[1024,128]{1,0:T(8,128)S(1)}, u32[]{:S(2)}, u32[]{:S(2)}) collective-permute-start(f32[1024,128]{1,0:T(8,128)} %sources_ref.1), channel_id=1, source_target_pairs={{0,128},{128,0},{1,129},{129,1},{2,130},{130,2},{3,131},{131,3},{4... | collective-permute-start | bytes 1572872 | tf_op jit(solution)/shard_map/ppermute | solution.py:285
  3.7 8.7 %collective-permute-start.1 = (f32[264,128]{1,0:T(8,128)S(1)}, f32[264,128]{1,0:T(8,128)S(1)}, u32[]{:S(2)}, u32[]{:S(2)}) collective-permute-start(f32[264,128]{1,0:T(8,128)S(1)} %select_maximum_fusion.block_ref.own_ref), channel_id=1, source_target_pairs={{0,16},{16,32},{32,48},{48,64},{64,80},{80,96},{96,112},{112,0},{1... | collective-permute-start | bytes 405512 | tf_op jit(solution)/shard_map/ppermute | solution.py:285
  5.4 7.0 %collective-permute-start.2 = (f32[264,128]{1,0:T(8,128)S(1)}, f32[264,128]{1,0:T(8,128)S(1)}, u32[]{:S(2)}, u32[]{:S(2)}) collective-permute-start(f32[264,128]{1,0:T(8,128)S(1)} %select_maximum_fusion.block_ref.own_ref), channel_id=1, source_target_pairs={{0,112},{16,0},{32,16},{48,32},{64,48},{80,64},{96,80},{112,96},{1... | collective-permute-start | bytes 405512 | tf_op jit(solution)/shard_map/ppermute | solution.py:285
  12.3 5.1 %collective-permute-start.3 = (f32[264,128]{1,0:T(8,128)S(1)}, f32[264,128]{1,0:T(8,128)S(1)}, u32[]{:S(2)}, u32[]{:S(2)}) collective-permute-start(f32[264,128]{1,0:T(8,128)S(1)} %collective-permute-done.1.lower_ref), channel_id=1, source_target_pairs={{0,16},{16,32},{32,48},{48,64},{64,80},{80,96},{96,112},{112,0},{1... | collective-permute-start | bytes 405512 | tf_op jit(solution)/shard_map/ppermute | solution.py:285
  12.3 7.0 %collective-permute-start.6 = (f32[264,128]{1,0:T(8,128)S(1)}, f32[264,128]{1,0:T(8,128)S(1)}, u32[]{:S(2)}, u32[]{:S(2)}) collective-permute-start(f32[264,128]{1,0:T(8,128)S(1)} %collective-permute-done.2.upper_ref), channel_id=1, source_target_pairs={{0,112},{16,0},{32,16},{48,32},{64,48},{80,64},{96,80},{112,96},{1... | collective-permute-start | bytes 405512 | tf_op jit(solution)/shard_map/ppermute | solution.py:285
  17.4 5.1 %collective-permute-start.4 = (f32[264,128]{1,0:T(8,128)S(1)}, f32[264,128]{1,0:T(8,128)S(1)}, u32[]{:S(2)}, u32[]{:S(2)}) collective-permute-start(f32[264,128]{1,0:T(8,128)S(1)} %collective-permute-done.3.refs_0_), channel_id=1, source_target_pairs={{0,16},{16,32},{32,48},{48,64},{64,80},{80,96},{96,112},{112,0},{1... | collective-permute-start | bytes 405512 | tf_op jit(solution)/shard_map/ppermute | solution.py:285
  17.4 1.0 %copy-start = (f32[1024,128]{1,0:T(8,128)S(1)}, f32[1024,128]{1,0:T(8,128)}, u32[]{:S(2)}) copy-start(f32[1024,128]{1,0:T(8,128)} %sources_ref.1) | copy-start | bytes 1572868
  19.3 8.2 %collective-permute-start.7 = (f32[264,128]{1,0:T(8,128)S(1)}, f32[264,128]{1,0:T(8,128)S(1)}, u32[]{:S(2)}, u32[]{:S(2)}) collective-permute-start(f32[264,128]{1,0:T(8,128)S(1)} %collective-permute-done.6.refs_1_), channel_id=1, source_target_pairs={{0,112},{16,0},{32,16},{48,32},{64,48},{80,64},{96,80},{112,96},{1... | collective-permute-start | bytes 405512 | tf_op jit(solution)/shard_map/ppermute | solution.py:285
  22.5 7.3 %collective-permute-start.5 = (f32[264,128]{1,0:T(8,128)S(1)}, f32[264,128]{1,0:T(8,128)S(1)}, u32[]{:S(2)}, u32[]{:S(2)}) collective-permute-start(f32[264,128]{1,0:T(8,128)S(1)} %collective-permute-done.4.refs_0_), channel_id=1, source_target_pairs={{0,16},{16,32},{32,48},{48,64},{64,80},{80,96},{96,112},{112,0},{1... | collective-permute-start | bytes 405512 | tf_op jit(solution)/shard_map/ppermute | solution.py:285

commit v3 on v2

--- a/solution.py
+++ b/solution.py
@@ -18,14 +18,14 @@
 ROWS = 1024
 COLS = 256
 RING = 8
-PLANE = 16
+PLANE = 32
 LANES = 128
 TILES = ROWS // LANES
 MIB = 1024 * 1024
 
 BLK = ("xl", "z")
 TGT = ("y", "xh", "core")
-PLANE_AXES = ("xl", "y", "xh")
+PLANE_AXES = ("xl", "y", "xh", "core")
 
 VMEM = pl.BlockSpec(memory_space=pltpu.VMEM)
 
@@ -121,6 +121,10 @@
             state_ref[0, half, :, tile], state_ref[1, half, :, tile] = state
 
 
+def ring_index(z, offset):
+    return lax.rem(z + (offset + RING), RING)
+
+
 def start_kernel(sources_ref, block_ref, tile_ref, x_ref, state_ref, src_norm_ref, dst_norm_ref, pots_scr):
     z, mine = lax.axis_index("z"), lax.axis_index("xl")
     eye = diagonal()
@@ -135,32 +139,38 @@
     add_block(parts, pots_scr, z, mine, x_ref, tile_ref, state_ref, True)
 
 
-def second_kernel(sources_ref, own_ref, lower_ref, upper_ref, *refs):
-    (tile_ref, x_ref, state_ref), pots_scr = refs[3:6], refs[6]
+def own_kernel(offsets, x_ref, *refs):
+    blocks, (tile_ref, state_ref), pots_scr = refs[: len(offsets)], refs[-3:-1], refs[-1]
     z, mine = lax.axis_index("z"), lax.axis_index("xl")
-    eye = diagonal()
-    prepare_sources(sources_ref[...], 1 - mine, x_ref)
-    for b, (block_ref, offset) in enumerate(((own_ref, 0), (lower_ref, -1), (upper_ref, 1))):
-        parts, _ = prepare_targets(eye, block_ref, pots_scr.at[b])
-        at = lax.rem(z + (offset + RING), RING)
-        if offset:
-            add_block(parts, pots_scr.at[b], at, mine, x_ref, tile_ref, state_ref, False)
-        add_block(parts, pots_scr.at[b], at, 1 - mine, x_ref, tile_ref, state_ref, not offset)
-
-
-def more_kernel(offsets, last, x_ref, *refs):
-    count = len(offsets)
-    blocks, (tile_ref, state_ref) = refs[:count], refs[count + 2 : count + 4]
-    pots_scr = refs[-1]
-    z = lax.axis_index("z")
     eye = diagonal()
     for b, offset in enumerate(offsets):
         parts, _ = prepare_targets(eye, blocks[b], pots_scr.at[b])
-        at = lax.rem(z + (offset + RING), RING)
-        for half in range(2):
-            add_block(parts, pots_scr.at[b], at, half, x_ref, tile_ref, state_ref, False)
-    if last:
-        put_rows(refs[count + 4], lambda half, tile: (state_ref[0, half, :, tile], state_ref[1, half, :, tile]))
+        add_block(parts, pots_scr.at[b], ring_index(z, offset), mine, x_ref, tile_ref, state_ref, False)
+
+
+def partner_kernel(fresh, work, *refs):
+    refs = list(refs)
+    sources_ref = refs.pop(0) if fresh else None
+    blocks, (tile_ref, x_ref, state_ref), pots_scr = refs[: len(work)], refs[-4:-1], refs[-1]
+    z, mine = lax.axis_index("z"), lax.axis_index("xl")
+    eye = diagonal()
+    if fresh:
+        prepare_sources(sources_ref[...], 1 - mine, x_ref)
+    for b, (offset, own, partner) in enumerate(work):
+        parts, _ = prepare_targets(eye, blocks[b], pots_scr.at[b])
+        at = ring_index(z, offset)
+        if own:
+            add_block(parts, pots_scr.at[b], at, mine, x_ref, tile_ref, state_ref, False)
+        if partner:
+            add_block(parts, pots_scr.at[b], at, 1 - mine, x_ref, tile_ref, state_ref, fresh and b == 0)
+
+
+def last_kernel(offset, x_ref, block_ref, *refs):
+    (tile_ref, state_ref, rows_ref), pots_scr = refs[-4:-1], refs[-1]
+    parts, _ = prepare_targets(diagonal(), block_ref, pots_scr)
+    for half in range(2):
+        add_block(parts, pots_scr, ring_index(lax.axis_index("z"), offset), half, x_ref, tile_ref, state_ref, False)
+    put_rows(rows_ref, lambda half, tile: (state_ref[0, half, :, tile], state_ref[1, half, :, tile]))
 
 
 F32 = jnp.float32
@@ -286,41 +296,48 @@
 
 
 def over_plane(copies):
-    return lax.all_gather(lax.all_to_all(copies, PLANE_AXES, 0, 0, tiled=True), "core", tiled=True)
+    return lax.all_to_all(copies, PLANE_AXES, 0, 0, tiled=True)
 
 
 def steps(sources, targets, duals_init):
     packed = jnp.concatenate([targets, jnp.pad(duals_init.reshape(2, LANES), ((0, 6), (0, 0)))], axis=0)
-    others = shifted(sources, "xl", 1)
     up, down = [packed], [packed]
     for step in range(1, RING // 2 + 1):
         up.append(shifted(up[-1], "z", 1))
         if step < RING // 2:
             down.append(shifted(down[-1], "z", -1))
+    others = shifted(sources, "xl", 1)
     pots = pltpu.VMEM((COLS, LANES), F32)
     norms = [jax.ShapeDtypeStruct((TILES, LANES), F32), jax.ShapeDtypeStruct((2, LANES), F32)]
     tile, x, state, src_norm, dst_norm = call(start_kernel, (sources, packed), [TILE, PARTS, STATE, *norms], 1, [pots])
+    tile, state = call(
+        functools.partial(own_kernel, (-1, 1)),
+        (x, up[1], down[1], tile, state),
+        [TILE, STATE],
+        2,
+        [pltpu.VMEM((2, COLS, LANES), F32)],
+        {3: 0, 4: 1},
+    )
     tile, x, state = call(
-        second_kernel,
-        (others, packed, up[1], down[1], tile, x, state),
+        functools.partial(partner_kernel, True, ((0, 0, 1), (-1, 0, 1), (1, 0, 1), (-2, 1, 0), (2, 1, 0))),
+        (others, packed, up[1], down[1], up[2], down[2], tile, x, state),
         [TILE, PARTS, STATE],
         5,
-        [pltpu.VMEM((3, COLS, LANES), F32)],
+        [pltpu.VMEM((5, COLS, LANES), F32)],
+        {6: 0, 7: 1, 8: 2},
+    )
+    tile, x, state = call(
+        functools.partial(partner_kernel, False, ((-2, 0, 1), (2, 0, 1), (-3, 1, 1), (3, 1, 1))),
+        (up[2], down[2], up[3], down[3], tile, x, state),
+        [TILE, PARTS, STATE],
+        6,
+        [pltpu.VMEM((4, COLS, LANES), F32)],
         {4: 0, 5: 1, 6: 2},
     )
-    for step in (2, 3, 4):
-        last = step == RING // 2
-        blocks = (up[step],) if last else (up[step], down[step])
-        offsets = (-step,) if last else (-step, step)
-        tile, state, *row_lse = call(
-            functools.partial(more_kernel, offsets, last),
-            (x, *blocks, tile, state),
-            [TILE, STATE] + [ROW_LSE] * last,
-            2 * len(blocks),
-            [pltpu.VMEM((2, COLS, LANES), F32)],
-            {1 + len(blocks): 0, 2 + len(blocks): 1},
-        )
-    (col_lse,) = columns(over_plane(row_lse[0]), src_norm, tile, True)
+    tile, state, row_lse = call(
+        functools.partial(last_kernel, -4), (x, up[4], tile, state), [TILE, STATE, ROW_LSE], 2, [pots], {2: 0, 3: 1}
+    )
+    (col_lse,) = columns(over_plane(row_lse), src_norm, tile, True)
     row_lse = rows(lax.all_to_all(col_lse, "z", 0, 0, tiled=True), tile)
     col_lse, source_pots = columns(over_plane(row_lse), src_norm, tile, False)
     col_lse = joined(lax.all_to_all(col_lse, "z", 0, 0, tiled=True))

time: 101 us -> 98.1 us (0.971)
  blocking collectives: 56.5 us -> 54.2 us
    all_gather x2 -> x0, blocking collectives: 11.7 us -> none  [over_plane(): lax.all_gather(lax.all_to_all(copies, PLANE_AXES, 0, 0, tiled=True), 'cor...]
    all_to_all x2, blocking collectives: 22.9 us -> 32.4 us  [over_plane(): return lax.all_to_all(copies, PLANE_AXES, 0, 0, tiled=True)]
  transfers between devices with their start and end apart: 8 -> 8, of which waited for: 3 -> 2; matrix products, arithmetic and copies ran while one was open for 1% -> 1% of each run, Pallas kernels for 8% -> 8%
where the time goes in v3:
time: 98.1 us; the launch traced here: 97.8 us
  blocking collectives  54.2 us (55%)
  Pallas kernels  21.6 us (22%)
  starting transfers between devices  13.3 us (14%)
  waiting for transfers between devices  5.33 us (5%)
  other arithmetic  1.56 us (2%)
  local copies, waits for them, and re-layouts  1.04 us (1%)
    all_to_all x2, blocking collectives, over_plane(): return lax.all_to_all(copies, PLANE_AXES, 0, 0, tiled=True)  32.4 us
    pallas_call x8, Pallas kernels, call(): pl.pallas_call(kernel, out_shape=outs, in_specs=[VMEM] * len(args), out_s...  21.6 us
    ppermute x8, starting transfers between devices, shifted(): return lax.ppermute(x, axis, [(i, (i + by) % count) for i in range(count)])  13.3 us
    all_to_all x1, blocking collectives, steps(): row_lse = rows(lax.all_to_all(col_lse, 'z', 0, 0, tiled=True), tile)  12.9 us
    all_to_all x1, blocking collectives, steps(): col_lse = joined(lax.all_to_all(col_lse, 'z', 0, 0, tiled=True))  8.94 us
    ppermute x8, waiting for transfers between devices, shifted(): return lax.ppermute(x, axis, [(i, (i + by) % count) for i in range(count)])  5.33 us
  transfers between devices with their start and end apart: 8, of which 2 were waited for; matrix products, arithmetic and copies ran while one was open for 1% of the time, Pallas kernels for 8%

profile of v3, /device:TPU:1, one launch (start us, length us, event | category | flops | bytes accessed | tf_op | source)
XLA Modules:
  0.0 97.8 jit_solution(9918451411520606905)
XLA Ops:
  0.6 2.1 %collective-permute-start.6 = (f32[1024,128]{1,0:T(8,128)}, f32[1024,128]{1,0:T(8,128)S(1)}, u32[]{:S(2)}, u32[]{:S(2)}) collective-permute-start(f32[1024,128]{1,0:T(8,128)} %sources_ref.1), channel_id=1, source_target_pairs={{0,128},{128,0},{1,129},{129,1},{2,130},{130,2},{3,131},{131,3},{4... | collective-permute-start | bytes 1572872 | tf_op jit(solution)/shard_map/ppermute | solution.py:295
  2.7 0.9 select_maximum_fusion.block_ref.refs_1_
  3.7 1.7 %collective-permute-start = (f32[264,128]{1,0:T(8,128)S(1)}, f32[264,128]{1,0:T(8,128)S(1)}, u32[]{:S(2)}, u32[]{:S(2)}) collective-permute-start(f32[264,128]{1,0:T(8,128)S(1)} %select_maximum_fusion.block_ref.refs_1_), channel_id=1, source_target_pairs={{0,16},{16,32},{32,48},{48,64},{64,80},{80,96},{96,112},{112,0},{1... | collective-permute-start | bytes 405512 | tf_op jit(solution)/shard_map/ppermute | solution.py:295
  5.4 4.0 %collective-permute-start.2 = (f32[264,128]{1,0:T(8,128)S(1)}, f32[264,128]{1,0:T(8,128)S(1)}, u32[]{:S(2)}, u32[]{:S(2)}) collective-permute-start(f32[264,128]{1,0:T(8,128)S(1)} %select_maximum_fusion.block_ref.refs_1_), channel_id=1, source_target_pairs={{0,112},{16,0},{32,16},{48,32},{64,48},{80,64},{96,80},{112,96},{1... | collective-permute-start | bytes 405512 | tf_op jit(solution)/shard_map/ppermute | solution.py:295
  9.4 2.9 %collective-permute-done.refs_0_.refs_2_ = f32[264,128]{1,0:T(8,128)S(1)} collective-permute-done((f32[264,128]{1,0:T(8,128)S(1)}, f32[264,128]{1,0:T(8,128)S(1)}, u32[]{:S(2)}, u32[]{:S(2)}) %collective-permute-start) | collective-permute-done | bytes 135200 | tf_op jit(solution)/shard_map/ppermute | solution.py:295
  12.3 0.0 collective-permute-start.1
  12.3 0.0 collective-permute-done.2.refs_1_.refs_3_
  12.3 2.7 %collective-permute-start.3 = (f32[264,128]{1,0:T(8,128)S(1)}, f32[264,128]{1,0:T(8,128)S(1)}, u32[]{:S(2)}, u32[]{:S(2)}) collective-permute-start(f32[264,128]{1,0:T(8,128)S(1)} %collective-permute-done.2.refs_1_.refs_3_), channel_id=1, source_target_pairs={{0,112},{16,0},{32,16},{48,32},{64,48},{80,64},{96,80},{112,96},{1... | collective-permute-start | bytes 405512 | tf_op jit(solution)/shard_map/ppermute | solution.py:295
  15.0 2.4 %collective-permute-done.1.refs_4_.refs_0_ = f32[264,128]{1,0:T(8,128)S(1)} collective-permute-done((f32[264,128]{1,0:T(8,128)S(1)}, f32[264,128]{1,0:T(8,128)S(1)}, u32[]{:S(2)}, u32[]{:S(2)}) %collective-permute-start.1) | collective-permute-done | bytes 135200 | tf_op jit(solution)/shard_map/ppermute | solution.py:295
  17.4 0.0 collective-permute-start.4
  17.4 0.0 copy-start
  17.4 1.0 %copy-done = f32[1024,128]{1,0:T(8,128)S(1)} copy-done((f32[1024,128]{1,0:T(8,128)S(1)}, f32[1024,128]{1,0:T(8,128)}, u32[]{:S(2)}) %copy-start) | copy-done | bytes 524312
  18.5 0.8 shard_map.50
  19.3 1.2 %shard_map.51 = (f32[8,2,256,1024]{3,2,1,0:T(8,128)S(1)}, f32[2,2,8,1024]{3,2,1,0:T(8,128)S(1)}) custom-call(bf16[2,768,1024]{2,1,0:T(8,128)(2,1)S(1)} %get-tuple-element.19.x_ref.refs_7_, f32[264,128]{1,0:T(8,128)S(1)} %collective-permute-done.refs_0_.refs_2_, ...), custom_call_target="tpu_custom_call", output_to_operand_aliasing={{0}: (3, {}), {1}: (4, {})} | custom-call | flops 805306368 | bytes 1048576 | tf_op jit(solution)/shard_map/pallas_call | solution.py:184
  20.5 0.0 collective-permute-done.3.refs_5_.refs_1_
  20.5 2.8 %collective-permute-start.5 = (f32[264,128]{1,0:T(8,128)S(1)}, f32[264,128]{1,0:T(8,128)S(1)}, u32[]{:S(2)}, u32[]{:S(2)}) collective-permute-start(f32[264,128]{1,0:T(8,128)S(1)} %collective-permute-done.3.refs_5_.refs_1_), channel_id=1, source_target_pairs={{0,112},{16,0},{32,16},{48,32},{64,48},{80,64},{96,80},{112,96},{1... | collective-permute-start | bytes 405512 | tf_op jit(solution)/shard_map/ppermute | solution.py:295
  23.3 0.0 collective-permute-done.4.refs_2_
  23.3 0.0 collective-permute-start.7
  23.3 0.0 collective-permute-done.6.refs_0_
  23.3 2.8 %shard_map.52 = (f32[8,2,256,1024]{3,2,1,0:T(8,128)S(1)}, bf16[2,768,1024]{2,1,0:T(8,128)(2,1)S(1)}, f32[2,2,8,1024]{3,2,1,0:T(8,128)S(1)}) custom-call(f32[1024,128]{1,0:T(8,128)S(1)} %collective-permute-done.6.refs_0_, f32[264,128]{1,0:T(8,128)S(1)} %select_maximum_fusion.block_ref.refs_1_, ...), custom_call_target="tpu_custom_call", output_to_operand_aliasing={{0}: (6, {}), {1}: (7, {}), {2}: (8, {})} | custom-call | flops 2013265920 | bytes 1048576 | tf_op jit(solution)/shard_map/pallas_call | solution.py:184
  26.2 0.0 collective-permute-done.5.refs_3_
  26.2 3.2 %shard_map.53 = (f32[8,2,256,1024]{3,2,1,0:T(8,128)S(1)}, bf16[2,768,1024]{2,1,0:T(8,128)(2,1)S(1)}, f32[2,2,8,1024]{3,2,1,0:T(8,128)S(1)}) custom-call(f32[264,128]{1,0:T(8,128)S(1)} %collective-permute-done.1.refs_4_.refs_0_, f32[264,128]{1,0:T(8,128)S(1)} %collective-permute-done.3.refs_5_.refs_1_, ...), custom_call_target="tpu_custom_call", output_to_operand_aliasing={{0}: (4, {}), {1}: (5, {}), {2}: (6, {})} | custom-call | flops 2415919104 | bytes 1048576 | tf_op jit(solution)/shard_map/pallas_call | solution.py:184
  29.4 0.0 collective-permute-done.7.block_ref
  29.4 1.3 %shard_map.54 = (f32[8,2,256,1024]{3,2,1,0:T(8,128)S(1)}, f32[2,2,8,1024]{3,2,1,0:T(8,128)S(1)}, f32[32,2,8,128]{3,2,1,0:T(8,128)S(1)}) custom-call(bf16[2,768,1024]{2,1,0:T(8,128)(2,1)S(1)} %get-tuple-element.27.x_ref, f32[264,128]{1,0:T(8,128)S(1)} %collective-permute-done.7.block_ref, ...), custom_call_target="tpu_custom_call", output_to_operand_aliasing={{0}: (2, {}), {1}: (3, {})} | custom-call | flops 805306368 | bytes 1048576 | tf_op jit(solution)/shard_map/pallas_call | solution.py:184
  30.7 18.6 %all_to_all.20.rows_ref = f32[32,2,8,128]{3,2,1,0:T(8,128)S(1)} all-to-all(f32[32,2,8,128]{3,2,1,0:T(8,128)S(1)} %get-tuple-element.30), channel_id=1, replica_groups=mesh['xl'=2,'z'=8,'y'=4,'xh'=2,'core'=2] {'xl','y','xh','core'}, dimensions={0} | all-to-all | bytes 524288 | tf_op jit(solution)/shard_map/all_to_all | solution.py:299
  49.3 4.1 %shard_map.55 = f32[8,16,128]{2,1,0:T(8,128)S(1)} custom-call(f32[32,2,8,128]{3,2,1,0:T(8,128)S(1)} %all_to_all.20.rows_ref, f32[8,128]{1,0:T(8,128)S(1)} %get-tuple-element.31.src_norm_ref, f32[8,2,256,1024]{3,2,1,0:T(8,128)S(1)} %get-tuple-element.32.tile_ref), custom_call_target="tpu_custom_call" | custom-call | flops 6442450944 | bytes 1048576 | tf_op jit(solution)/shard_map/pallas_call | solution.py:184
  53.4 12.9 %all_to_all.21.cols_ref = f32[8,16,128]{2,1,0:T(8,128)S(1)} all-to-all(f32[8,16,128]{2,1,0:T(8,128)S(1)} %shard_map.55), channel_id=1, replica_groups=mesh['xl'=2,'z'=8,'y'=4,'xh'=2,'core'=2] {'z'}, dimensions={0} | all-to-all | bytes 131072 | tf_op jit(solution)/shard_map/all_to_all | solution.py:341
  66.3 4.0 %shard_map.56 = f32[32,2,8,128]{3,2,1,0:T(8,128)S(1)} custom-call(f32[8,16,128]{2,1,0:T(8,128)S(1)} %all_to_all.21.cols_ref, f32[8,2,256,1024]{3,2,1,0:T(8,128)S(1)} %get-tuple-element.32.tile_ref), custom_call_target="tpu_custom_call" | custom-call | flops 6442450944 | bytes 1048576 | tf_op jit(solution)/shard_map/pallas_call | solution.py:184
  70.3 13.8 %all_to_all.22.rows_ref = f32[32,2,8,128]{3,2,1,0:T(8,128)S(1)} all-to-all(f32[32,2,8,128]{3,2,1,0:T(8,128)S(1)} %shard_map.56), channel_id=1, replica_groups=mesh['xl'=2,'z'=8,'y'=4,'xh'=2,'core'=2] {'xl','y','xh','core'}, dimensions={0} | all-to-all | bytes 524288 | tf_op jit(solution)/shard_map/all_to_all | solution.py:299
  84.1 4.1 %shard_map.57 = (f32[8,2,128]{2,1,0:T(2,128)S(1)}, f32[8,128]{1,0:T(8,128)}) custom-call(f32[32,2,8,128]{3,2,1,0:T(8,128)S(1)} %all_to_all.22.rows_ref, f32[8,128]{1,0:T(8,128)S(1)} %get-tuple-element.31.src_norm_ref, f32[8,2,256,1024]{3,2,1,0:T(8,128)S(1)} %get-tuple-element.32.tile_ref), custom_call_target="tpu_custom_call" | custom-call | flops 6442450944 | bytes 1048576 | tf_op jit(solution)/shard_map/pallas_call | solution.py:184
  88.2 8.9 %all_to_all.23 = f32[8,2,128]{2,1,0:T(2,128)S(1)} all-to-all(f32[8,2,128]{2,1,0:T(2,128)S(1)} %get-tuple-element.34), channel_id=1, replica_groups=mesh['xl'=2,'z'=8,'y'=4,'xh'=2,'core'=2] {'z'}, dimensions={0} | all-to-all | bytes 16384 | tf_op jit(solution)/shard_map/all_to_all | solution.py:343
  97.2 0.6 add_bitcast_fusion
  (2 shorter events, 0.0 us)
Async XLA Ops:
  0.6 22.7 %collective-permute-start.6 = (f32[1024,128]{1,0:T(8,128)}, f32[1024,128]{1,0:T(8,128)S(1)}, u32[]{:S(2)}, u32[]{:S(2)}) collective-permute-start(f32[1024,128]{1,0:T(8,128)} %sources_ref.1), channel_id=1, source_target_pairs={{0,128},{128,0},{1,129},{129,1},{2,130},{130,2},{3,131},{131,3},{4... | collective-permute-start | bytes 1572872 | tf_op jit(solution)/shard_map/ppermute | solution.py:295
  3.7 8.7 %collective-permute-start = (f32[264,128]{1,0:T(8,128)S(1)}, f32[264,128]{1,0:T(8,128)S(1)}, u32[]{:S(2)}, u32[]{:S(2)}) collective-permute-start(f32[264,128]{1,0:T(8,128)S(1)} %select_maximum_fusion.block_ref.refs_1_), channel_id=1, source_target_pairs={{0,16},{16,32},{32,48},{48,64},{64,80},{80,96},{96,112},{112,0},{1... | collective-permute-start | bytes 405512 | tf_op jit(solution)/shard_map/ppermute | solution.py:295
  5.4 7.0 %collective-permute-start.2 = (f32[264,128]{1,0:T(8,128)S(1)}, f32[264,128]{1,0:T(8,128)S(1)}, u32[]{:S(2)}, u32[]{:S(2)}) collective-permute-start(f32[264,128]{1,0:T(8,128)S(1)} %select_maximum_fusion.block_ref.refs_1_), channel_id=1, source_target_pairs={{0,112},{16,0},{32,16},{48,32},{64,48},{80,64},{96,80},{112,96},{1... | collective-permute-start | bytes 405512 | tf_op jit(solution)/shard_map/ppermute | solution.py:295
  12.3 5.1 %collective-permute-start.1 = (f32[264,128]{1,0:T(8,128)S(1)}, f32[264,128]{1,0:T(8,128)S(1)}, u32[]{:S(2)}, u32[]{:S(2)}) collective-permute-start(f32[264,128]{1,0:T(8,128)S(1)} %collective-permute-done.refs_0_.refs_2_), channel_id=1, source_target_pairs={{0,16},{16,32},{32,48},{48,64},{64,80},{80,96},{96,112},{112,0},{1... | collective-permute-start | bytes 405512 | tf_op jit(solution)/shard_map/ppermute | solution.py:295
  12.3 8.2 %collective-permute-start.3 = (f32[264,128]{1,0:T(8,128)S(1)}, f32[264,128]{1,0:T(8,128)S(1)}, u32[]{:S(2)}, u32[]{:S(2)}) collective-permute-start(f32[264,128]{1,0:T(8,128)S(1)} %collective-permute-done.2.refs_1_.refs_3_), channel_id=1, source_target_pairs={{0,112},{16,0},{32,16},{48,32},{64,48},{80,64},{96,80},{112,96},{1... | collective-permute-start | bytes 405512 | tf_op jit(solution)/shard_map/ppermute | solution.py:295
  17.4 5.9 %collective-permute-start.4 = (f32[264,128]{1,0:T(8,128)S(1)}, f32[264,128]{1,0:T(8,128)S(1)}, u32[]{:S(2)}, u32[]{:S(2)}) collective-permute-start(f32[264,128]{1,0:T(8,128)S(1)} %collective-permute-done.1.refs_4_.refs_0_), channel_id=1, source_target_pairs={{0,16},{16,32},{32,48},{48,64},{64,80},{80,96},{96,112},{112,0},{1... | collective-permute-start | bytes 405512 | tf_op jit(solution)/shard_map/ppermute | solution.py:295
  17.4 1.0 %copy-start = (f32[1024,128]{1,0:T(8,128)S(1)}, f32[1024,128]{1,0:T(8,128)}, u32[]{:S(2)}) copy-start(f32[1024,128]{1,0:T(8,128)} %sources_ref.1) | copy-start | bytes 1572868
  20.5 5.6 %collective-permute-start.5 = (f32[264,128]{1,0:T(8,128)S(1)}, f32[264,128]{1,0:T(8,128)S(1)}, u32[]{:S(2)}, u32[]{:S(2)}) collective-permute-start(f32[264,128]{1,0:T(8,128)S(1)} %collective-permute-done.3.refs_5_.refs_1_), channel_id=1, source_target_pairs={{0,112},{16,0},{32,16},{48,32},{64,48},{80,64},{96,80},{112,96},{1... | collective-permute-start | bytes 405512 | tf_op jit(solution)/shard_map/ppermute | solution.py:295
  23.3 6.1 %collective-permute-start.7 = (f32[264,128]{1,0:T(8,128)S(1)}, f32[264,128]{1,0:T(8,128)S(1)}, u32[]{:S(2)}, u32[]{:S(2)}) collective-permute-start(f32[264,128]{1,0:T(8,128)S(1)} %collective-permute-done.4.refs_2_), channel_id=1, source_target_pairs={{0,16},{16,32},{32,48},{48,64},{64,80},{80,96},{96,112},{112,0},{1... | collective-permute-start | bytes 405512 | tf_op jit(solution)/shard_map/ppermute | solution.py:295

commit v4 on v3

--- a/solution.py
+++ b/solution.py
@@ -212,19 +212,18 @@
     def finish(k):
         for c in range(COLS // LANES):
             rows = slice(c * LANES, (c + 1) * LANES)
-            high, total = high_scr[rows, :].T, total_scr[rows, :].T
-            top = jnp.max(high, axis=0, keepdims=True)
-            lse_scr[k, c : c + 1, :] = top + log2(jnp.sum(total * jnp.exp2(high - top), axis=0, keepdims=True))
+            highs = [high_scr[h, rows, :].T for h in range(2)]
+            top = jnp.max(jnp.maximum(*highs), axis=0, keepdims=True)
+            total = sum(total_scr[h, rows, :].T * jnp.exp2(highs[h] - top) for h in range(2))
+            lse_scr[k, c : c + 1, :] = top + log2(jnp.sum(total, axis=0, keepdims=True))
 
     def block(k, carry):
         finish(jnp.maximum(k - 1, 0))
-        for r in range(0, COLS, 8):
-            scores = [
-                tile_ref[k, h, r : r + 8, t * LANES : (t + 1) * LANES] + pots[h * TILES + t]
-                for h in range(2)
-                for t in range(TILES)
-            ]
-            high_scr[r : r + 8, :], total_scr[r : r + 8, :] = online(scores, None)
+        for h in range(2):
+            for r in range(0, COLS, 8):
+                tiles = [slice(t * LANES, (t + 1) * LANES) for t in range(TILES)]
+                scores = [tile_ref[k, h, r : r + 8, tiles[t]] + pots[h * TILES + t] for t in range(TILES)]
+                high_scr[h, r : r + 8, :], total_scr[h, r : r + 8, :] = online(scores, None)
         return carry
 
     lax.fori_loop(0, RING, block, 0)
@@ -242,7 +241,7 @@
         outs = [jax.ShapeDtypeStruct((RING, RING * 2, LANES), F32)]
     else:
         outs = [jax.ShapeDtypeStruct((RING, 2, LANES), F32), jax.ShapeDtypeStruct((TILES, LANES), F32)]
-    scratch = [pltpu.VMEM((COLS, LANES), F32)] * 2 + [pltpu.VMEM((RING, 2, LANES), F32)]
+    scratch = [pltpu.VMEM((2, COLS, LANES), F32)] * 2 + [pltpu.VMEM((RING, 2, LANES), F32)]
     return call(functools.partial(columns_kernel, copies), (rows, src_norm, tile), outs, 16, scratch)
 
 
@@ -301,39 +300,43 @@
 
 def steps(sources, targets, duals_init):
     packed = jnp.concatenate([targets, jnp.pad(duals_init.reshape(2, LANES), ((0, 6), (0, 0)))], axis=0)
+    others = shifted(sources, "xl", 1)
     up, down = [packed], [packed]
     for step in range(1, RING // 2 + 1):
         up.append(shifted(up[-1], "z", 1))
         if step < RING // 2:
             down.append(shifted(down[-1], "z", -1))
-    others = shifted(sources, "xl", 1)
     pots = pltpu.VMEM((COLS, LANES), F32)
     norms = [jax.ShapeDtypeStruct((TILES, LANES), F32), jax.ShapeDtypeStruct((2, LANES), F32)]
     tile, x, state, src_norm, dst_norm = call(start_kernel, (sources, packed), [TILE, PARTS, STATE, *norms], 1, [pots])
-    tile, state = call(
-        functools.partial(own_kernel, (-1, 1)),
-        (x, up[1], down[1], tile, state),
-        [TILE, STATE],
-        2,
-        [pltpu.VMEM((2, COLS, LANES), F32)],
-        {3: 0, 4: 1},
-    )
-    tile, x, state = call(
-        functools.partial(partner_kernel, True, ((0, 0, 1), (-1, 0, 1), (1, 0, 1), (-2, 1, 0), (2, 1, 0))),
-        (others, packed, up[1], down[1], up[2], down[2], tile, x, state),
-        [TILE, PARTS, STATE],
-        5,
-        [pltpu.VMEM((5, COLS, LANES), F32)],
-        {6: 0, 7: 1, 8: 2},
-    )
-    tile, x, state = call(
-        functools.partial(partner_kernel, False, ((-2, 0, 1), (2, 0, 1), (-3, 1, 1), (3, 1, 1))),
-        (up[2], down[2], up[3], down[3], tile, x, state),
-        [TILE, PARTS, STATE],
-        6,
-        [pltpu.VMEM((4, COLS, LANES), F32)],
-        {4: 0, 5: 1, 6: 2},
-    )
+
+    def own(step):
+        return call(
+            functools.partial(own_kernel, (-step, step)),
+            (x, up[step], down[step], tile, state),
+            [TILE, STATE],
+            2,
+            [pltpu.VMEM((2, COLS, LANES), F32)],
+            {3: 0, 4: 1},
+        )
+
+    def partner(fresh, work, *blocks):
+        first = (others,) if fresh else ()
+        at = len(first) + len(blocks)
+        return call(
+            functools.partial(partner_kernel, fresh, work),
+            (*first, *blocks, tile, x, state),
+            [TILE, PARTS, STATE],
+            sum(a + b for _, a, b in work),
+            [pltpu.VMEM((len(work), COLS, LANES), F32)],
+            {at: 0, at + 1: 1, at + 2: 2},
+        )
+
+    tile, state = own(1)
+    tile, state = own(2)
+    tile, x, state = partner(True, ((0, 0, 1), (-1, 0, 1), (1, 0, 1)), packed, up[1], down[1])
+    work = ((-2, 0, 1), (2, 0, 1), (-3, 1, 1), (3, 1, 1))
+    tile, x, state = partner(False, work, up[2], down[2], up[3], down[3])
     tile, state, row_lse = call(
         functools.partial(last_kernel, -4), (x, up[4], tile, state), [TILE, STATE, ROW_LSE], 2, [pots], {2: 0, 3: 1}
     )

time: 98.1 us -> 97.3 us (level)
  waiting for transfers between devices: 5.33 us -> 3.44 us
    ppermute x8, waiting for transfers between devices: 5.33 us -> 3.44 us  [shifted(): return lax.ppermute(x, axis, [(i, (i + by) % count) for i in range(count)])]
    all_to_all x2, blocking collectives: 32.4 us -> 33.6 us  [over_plane(): return lax.all_to_all(copies, PLANE_AXES, 0, 0, tiled=True)]
    pallas_call x8 -> x9, Pallas kernels: 21.6 us -> 21.9 us  [call(): pl.pallas_call(kernel, out_shape=outs, in_specs=[VMEM] * len(args), out_s...]
  transfers between devices with their start and end apart: 8 -> 8, of which waited for: 2 -> 2; matrix products, arithmetic and copies ran while one was open for 1% -> 1% of each run, Pallas kernels for 8% -> 9%
where the time goes in v4:
time: 97.3 us; the launch traced here: 97 us
  blocking collectives  54.8 us (56%)
  Pallas kernels  21.9 us (23%)
  starting transfers between devices  13.5 us (14%)
  waiting for transfers between devices  3.44 us (4%)
  other arithmetic  1.56 us (2%)
  local copies, waits for them, and re-layouts  1.04 us (1%)
    all_to_all x2, blocking collectives, over_plane(): return lax.all_to_all(copies, PLANE_AXES, 0, 0, tiled=True)  33.6 us
    pallas_call x9, Pallas kernels, call(): pl.pallas_call(kernel, out_shape=outs, in_specs=[VMEM] * len(args), out_s...  21.9 us
    ppermute x8, starting transfers between devices, shifted(): return lax.ppermute(x, axis, [(i, (i + by) % count) for i in range(count)])  13.5 us
    all_to_all x1, blocking collectives, steps(): row_lse = rows(lax.all_to_all(col_lse, 'z', 0, 0, tiled=True), tile)  12.3 us
    all_to_all x1, blocking collectives, steps(): col_lse = joined(lax.all_to_all(col_lse, 'z', 0, 0, tiled=True))  8.94 us
    ppermute x8, waiting for transfers between devices, shifted(): return lax.ppermute(x, axis, [(i, (i + by) % count) for i in range(count)])  3.44 us
  transfers between devices with their start and end apart: 8, of which 2 were waited for; matrix products, arithmetic and copies ran while one was open for 1% of the time, Pallas kernels for 9%

profile of v4, /device:TPU:1, one launch (start us, length us, event | category | flops | bytes accessed | tf_op | source)
XLA Modules:
  0.0 97.0 jit_solution(10231841672712726752)
XLA Ops:
  0.6 2.1 %collective-permute-start.6 = (f32[1024,128]{1,0:T(8,128)}, f32[1024,128]{1,0:T(8,128)S(1)}, u32[]{:S(2)}, u32[]{:S(2)}) collective-permute-start(f32[1024,128]{1,0:T(8,128)} %sources_ref.1), channel_id=1, source_target_pairs={{0,128},{128,0},{1,129},{129,1},{2,130},{130,2},{3,131},{131,3},{4... | collective-permute-start | bytes 1572872 | tf_op jit(solution)/shard_map/ppermute | solution.py:294
  2.7 0.9 select_maximum_fusion.block_ref.refs_1_
  3.7 1.7 %collective-permute-start = (f32[264,128]{1,0:T(8,128)S(1)}, f32[264,128]{1,0:T(8,128)S(1)}, u32[]{:S(2)}, u32[]{:S(2)}) collective-permute-start(f32[264,128]{1,0:T(8,128)S(1)} %select_maximum_fusion.block_ref.refs_1_), channel_id=1, source_target_pairs={{0,16},{16,32},{32,48},{48,64},{64,80},{80,96},{96,112},{112,0},{1... | collective-permute-start | bytes 405512 | tf_op jit(solution)/shard_map/ppermute | solution.py:294
  5.4 4.0 %collective-permute-start.2 = (f32[264,128]{1,0:T(8,128)S(1)}, f32[264,128]{1,0:T(8,128)S(1)}, u32[]{:S(2)}, u32[]{:S(2)}) collective-permute-start(f32[264,128]{1,0:T(8,128)S(1)} %select_maximum_fusion.block_ref.refs_1_), channel_id=1, source_target_pairs={{0,112},{16,0},{32,16},{48,32},{64,48},{80,64},{96,80},{112,96},{1... | collective-permute-start | bytes 405512 | tf_op jit(solution)/shard_map/ppermute | solution.py:294
  9.4 2.9 %collective-permute-done.refs_0_.refs_2_ = f32[264,128]{1,0:T(8,128)S(1)} collective-permute-done((f32[264,128]{1,0:T(8,128)S(1)}, f32[264,128]{1,0:T(8,128)S(1)}, u32[]{:S(2)}, u32[]{:S(2)}) %collective-permute-start) | collective-permute-done | bytes 135200 | tf_op jit(solution)/shard_map/ppermute | solution.py:294
  12.3 0.0 collective-permute-start.1
  12.3 0.0 collective-permute-done.2.refs_1_.refs_3_
  12.3 2.7 %collective-permute-start.3 = (f32[264,128]{1,0:T(8,128)S(1)}, f32[264,128]{1,0:T(8,128)S(1)}, u32[]{:S(2)}, u32[]{:S(2)}) collective-permute-start(f32[264,128]{1,0:T(8,128)S(1)} %collective-permute-done.2.refs_1_.refs_3_), channel_id=1, source_target_pairs={{0,112},{16,0},{32,16},{48,32},{64,48},{80,64},{96,80},{112,96},{1... | collective-permute-start | bytes 405512 | tf_op jit(solution)/shard_map/ppermute | solution.py:294
  15.0 1.0 %copy-done = f32[1024,128]{1,0:T(8,128)S(1)} copy-done((f32[1024,128]{1,0:T(8,128)S(1)}, f32[1024,128]{1,0:T(8,128)}, u32[]{:S(2)}) %copy-start) | copy-done | bytes 524312
  16.1 0.8 shard_map.50
  16.9 0.5 collective-permute-done.1.refs_0_
  17.4 0.0 collective-permute-start.4
  17.4 1.2 %shard_map.51 = (f32[8,2,256,1024]{3,2,1,0:T(8,128)S(1)}, f32[2,2,8,1024]{3,2,1,0:T(8,128)S(1)}) custom-call(bf16[2,768,1024]{2,1,0:T(8,128)(2,1)S(1)} %get-tuple-element.21.x_ref.refs_5_, f32[264,128]{1,0:T(8,128)S(1)} %collective-permute-done.refs_0_.refs_2_, ...), custom_call_target="tpu_custom_call", output_to_operand_aliasing={{0}: (3, {}), {1}: (4, {})} | custom-call | flops 805306368 | bytes 1048576 | tf_op jit(solution)/shard_map/pallas_call | solution.py:184
  18.6 0.0 collective-permute-done.3.refs_1_
  18.7 2.7 %collective-permute-start.5 = (f32[264,128]{1,0:T(8,128)S(1)}, f32[264,128]{1,0:T(8,128)S(1)}, u32[]{:S(2)}, u32[]{:S(2)}) collective-permute-start(f32[264,128]{1,0:T(8,128)S(1)} %collective-permute-done.3.refs_1_), channel_id=1, source_target_pairs={{0,112},{16,0},{32,16},{48,32},{64,48},{80,64},{96,80},{112,96},{1... | collective-permute-start | bytes 405512 | tf_op jit(solution)/shard_map/ppermute | solution.py:294
  21.4 1.2 %shard_map.52 = (f32[8,2,256,1024]{3,2,1,0:T(8,128)S(1)}, f32[2,2,8,1024]{3,2,1,0:T(8,128)S(1)}) custom-call(bf16[2,768,1024]{2,1,0:T(8,128)(2,1)S(1)} %get-tuple-element.21.x_ref.refs_5_, f32[264,128]{1,0:T(8,128)S(1)} %collective-permute-done.1.refs_0_, ...), custom_call_target="tpu_custom_call", output_to_operand_aliasing={{0}: (3, {}), {1}: (4, {})} | custom-call | flops 805306368 | bytes 1048576 | tf_op jit(solution)/shard_map/pallas_call | solution.py:184
  22.6 0.0 collective-permute-done.4.refs_2_
  22.6 0.3 collective-permute-start.7
  22.9 0.0 collective-permute-done.6.refs_0_
  22.9 1.8 %shard_map.53 = (f32[8,2,256,1024]{3,2,1,0:T(8,128)S(1)}, bf16[2,768,1024]{2,1,0:T(8,128)(2,1)S(1)}, f32[2,2,8,1024]{3,2,1,0:T(8,128)S(1)}) custom-call(f32[1024,128]{1,0:T(8,128)S(1)} %collective-permute-done.6.refs_0_, f32[264,128]{1,0:T(8,128)S(1)} %select_maximum_fusion.block_ref.refs_1_, ...), custom_call_target="tpu_custom_call", output_to_operand_aliasing={{0}: (4, {}), {1}: (5, {}), {2}: (6, {})} | custom-call | flops 1207959552 | bytes 1048576 | tf_op jit(solution)/shard_map/pallas_call | solution.py:184
  24.8 0.0 collective-permute-done.5.refs_3_
  24.8 3.3 %shard_map.54 = (f32[8,2,256,1024]{3,2,1,0:T(8,128)S(1)}, bf16[2,768,1024]{2,1,0:T(8,128)(2,1)S(1)}, f32[2,2,8,1024]{3,2,1,0:T(8,128)S(1)}) custom-call(f32[264,128]{1,0:T(8,128)S(1)} %collective-permute-done.1.refs_0_, f32[264,128]{1,0:T(8,128)S(1)} %collective-permute-done.3.refs_1_, ...), custom_call_target="tpu_custom_call", output_to_operand_aliasing={{0}: (4, {}), {1}: (5, {}), {2}: (6, {})} | custom-call | flops 2415919104 | bytes 1048576 | tf_op jit(solution)/shard_map/pallas_call | solution.py:184
  28.0 0.0 collective-permute-done.7.block_ref
  28.0 1.3 %shard_map.55 = (f32[8,2,256,1024]{3,2,1,0:T(8,128)S(1)}, f32[2,2,8,1024]{3,2,1,0:T(8,128)S(1)}, f32[32,2,8,128]{3,2,1,0:T(8,128)S(1)}) custom-call(bf16[2,768,1024]{2,1,0:T(8,128)(2,1)S(1)} %get-tuple-element.31.x_ref, f32[264,128]{1,0:T(8,128)S(1)} %collective-permute-done.7.block_ref, ...), custom_call_target="tpu_custom_call", output_to_operand_aliasing={{0}: (2, {}), {1}: (3, {})} | custom-call | flops 805306368 | bytes 1048576 | tf_op jit(solution)/shard_map/pallas_call | solution.py:184
  29.3 19.8 %all_to_all.20.rows_ref = f32[32,2,8,128]{3,2,1,0:T(8,128)S(1)} all-to-all(f32[32,2,8,128]{3,2,1,0:T(8,128)S(1)} %get-tuple-element.34), channel_id=1, replica_groups=mesh['xl'=2,'z'=8,'y'=4,'xh'=2,'core'=2] {'xl','y','xh','core'}, dimensions={0} | all-to-all | bytes 524288 | tf_op jit(solution)/shard_map/all_to_all | solution.py:298
  49.1 4.2 %shard_map.56 = f32[8,16,128]{2,1,0:T(8,128)S(1)} custom-call(f32[32,2,8,128]{3,2,1,0:T(8,128)S(1)} %all_to_all.20.rows_ref, f32[8,128]{1,0:T(8,128)S(1)} %get-tuple-element.35.src_norm_ref, f32[8,2,256,1024]{3,2,1,0:T(8,128)S(1)} %get-tuple-element.36.tile_ref), custom_call_target="tpu_custom_call" | custom-call | flops 6442450944 | bytes 1048576 | tf_op jit(solution)/shard_map/pallas_call | solution.py:184
  53.2 12.3 %all_to_all.21.cols_ref = f32[8,16,128]{2,1,0:T(8,128)S(1)} all-to-all(f32[8,16,128]{2,1,0:T(8,128)S(1)} %shard_map.56), channel_id=1, replica_groups=mesh['xl'=2,'z'=8,'y'=4,'xh'=2,'core'=2] {'z'}, dimensions={0} | all-to-all | bytes 131072 | tf_op jit(solution)/shard_map/all_to_all | solution.py:344
  65.5 4.0 %shard_map.57 = f32[32,2,8,128]{3,2,1,0:T(8,128)S(1)} custom-call(f32[8,16,128]{2,1,0:T(8,128)S(1)} %all_to_all.21.cols_ref, f32[8,2,256,1024]{3,2,1,0:T(8,128)S(1)} %get-tuple-element.36.tile_ref), custom_call_target="tpu_custom_call" | custom-call | flops 6442450944 | bytes 1048576 | tf_op jit(solution)/shard_map/pallas_call | solution.py:184
  69.6 13.8 %all_to_all.22.rows_ref = f32[32,2,8,128]{3,2,1,0:T(8,128)S(1)} all-to-all(f32[32,2,8,128]{3,2,1,0:T(8,128)S(1)} %shard_map.57), channel_id=1, replica_groups=mesh['xl'=2,'z'=8,'y'=4,'xh'=2,'core'=2] {'xl','y','xh','core'}, dimensions={0} | all-to-all | bytes 524288 | tf_op jit(solution)/shard_map/all_to_all | solution.py:298
  83.4 4.1 %shard_map.58 = (f32[8,2,128]{2,1,0:T(2,128)S(1)}, f32[8,128]{1,0:T(8,128)}) custom-call(f32[32,2,8,128]{3,2,1,0:T(8,128)S(1)} %all_to_all.22.rows_ref, f32[8,128]{1,0:T(8,128)S(1)} %get-tuple-element.35.src_norm_ref, f32[8,2,256,1024]{3,2,1,0:T(8,128)S(1)} %get-tuple-element.36.tile_ref), custom_call_target="tpu_custom_call" | custom-call | flops 6442450944 | bytes 1048576 | tf_op jit(solution)/shard_map/pallas_call | solution.py:184
  87.5 8.9 %all_to_all.23 = f32[8,2,128]{2,1,0:T(2,128)S(1)} all-to-all(f32[8,2,128]{2,1,0:T(2,128)S(1)} %get-tuple-element.38), channel_id=1, replica_groups=mesh['xl'=2,'z'=8,'y'=4,'xh'=2,'core'=2] {'z'}, dimensions={0} | all-to-all | bytes 16384 | tf_op jit(solution)/shard_map/all_to_all | solution.py:346
  96.5 0.6 add_bitcast_fusion
  (3 shorter events, 0.0 us)
Async XLA Ops:
  0.6 22.3 %collective-permute-start.6 = (f32[1024,128]{1,0:T(8,128)}, f32[1024,128]{1,0:T(8,128)S(1)}, u32[]{:S(2)}, u32[]{:S(2)}) collective-permute-start(f32[1024,128]{1,0:T(8,128)} %sources_ref.1), channel_id=1, source_target_pairs={{0,128},{128,0},{1,129},{129,1},{2,130},{130,2},{3,131},{131,3},{4... | collective-permute-start | bytes 1572872 | tf_op jit(solution)/shard_map/ppermute | solution.py:294
  3.7 8.7 %collective-permute-start = (f32[264,128]{1,0:T(8,128)S(1)}, f32[264,128]{1,0:T(8,128)S(1)}, u32[]{:S(2)}, u32[]{:S(2)}) collective-permute-start(f32[264,128]{1,0:T(8,128)S(1)} %select_maximum_fusion.block_ref.refs_1_), channel_id=1, source_target_pairs={{0,16},{16,32},{32,48},{48,64},{64,80},{80,96},{96,112},{112,0},{1... | collective-permute-start | bytes 405512 | tf_op jit(solution)/shard_map/ppermute | solution.py:294
  5.4 7.0 %collective-permute-start.2 = (f32[264,128]{1,0:T(8,128)S(1)}, f32[264,128]{1,0:T(8,128)S(1)}, u32[]{:S(2)}, u32[]{:S(2)}) collective-permute-start(f32[264,128]{1,0:T(8,128)S(1)} %select_maximum_fusion.block_ref.refs_1_), channel_id=1, source_target_pairs={{0,112},{16,0},{32,16},{48,32},{64,48},{80,64},{96,80},{112,96},{1... | collective-permute-start | bytes 405512 | tf_op jit(solution)/shard_map/ppermute | solution.py:294
  12.3 5.1 %collective-permute-start.1 = (f32[264,128]{1,0:T(8,128)S(1)}, f32[264,128]{1,0:T(8,128)S(1)}, u32[]{:S(2)}, u32[]{:S(2)}) collective-permute-start(f32[264,128]{1,0:T(8,128)S(1)} %collective-permute-done.refs_0_.refs_2_), channel_id=1, source_target_pairs={{0,16},{16,32},{32,48},{48,64},{64,80},{80,96},{96,112},{112,0},{1... | collective-permute-start | bytes 405512 | tf_op jit(solution)/shard_map/ppermute | solution.py:294
  12.3 6.3 %collective-permute-start.3 = (f32[264,128]{1,0:T(8,128)S(1)}, f32[264,128]{1,0:T(8,128)S(1)}, u32[]{:S(2)}, u32[]{:S(2)}) collective-permute-start(f32[264,128]{1,0:T(8,128)S(1)} %collective-permute-done.2.refs_1_.refs_3_), channel_id=1, source_target_pairs={{0,112},{16,0},{32,16},{48,32},{64,48},{80,64},{96,80},{112,96},{1... | collective-permute-start | bytes 405512 | tf_op jit(solution)/shard_map/ppermute | solution.py:294
  15.0 1.0 %copy-start = (f32[1024,128]{1,0:T(8,128)S(1)}, f32[1024,128]{1,0:T(8,128)}, u32[]{:S(2)}) copy-start(f32[1024,128]{1,0:T(8,128)} %sources_ref.1) | copy-start | bytes 1572868
  17.4 5.2 %collective-permute-start.4 = (f32[264,128]{1,0:T(8,128)S(1)}, f32[264,128]{1,0:T(8,128)S(1)}, u32[]{:S(2)}, u32[]{:S(2)}) collective-permute-start(f32[264,128]{1,0:T(8,128)S(1)} %collective-permute-done.1.refs_0_), channel_id=1, source_target_pairs={{0,16},{16,32},{32,48},{48,64},{64,80},{80,96},{96,112},{112,0},{1... | collective-permute-start | bytes 405512 | tf_op jit(solution)/shard_map/ppermute | solution.py:294
  18.7 6.1 %collective-permute-start.5 = (f32[264,128]{1,0:T(8,128)S(1)}, f32[264,128]{1,0:T(8,128)S(1)}, u32[]{:S(2)}, u32[]{:S(2)}) collective-permute-start(f32[264,128]{1,0:T(8,128)S(1)} %collective-permute-done.3.refs_1_), channel_id=1, source_target_pairs={{0,112},{16,0},{32,16},{48,32},{64,48},{80,64},{96,80},{112,96},{1... | collective-permute-start | bytes 405512 | tf_op jit(solution)/shard_map/ppermute | solution.py:294
  22.6 5.4 %collective-permute-start.7 = (f32[264,128]{1,0:T(8,128)S(1)}, f32[264,128]{1,0:T(8,128)S(1)}, u32[]{:S(2)}, u32[]{:S(2)}) collective-permute-start(f32[264,128]{1,0:T(8,128)S(1)} %collective-permute-done.4.refs_2_), channel_id=1, source_target_pairs={{0,16},{16,32},{32,48},{48,64},{64,80},{80,96},{96,112},{112,0},{1... | collective-permute-start | bytes 405512 | tf_op jit(solution)/shard_map/ppermute | solution.py:294
